TPU v7x, 128 devices: a whole 4x4x4 slice. The times are simulated.
128 devices in a mesh: mem: 8 (over z, core), space: 16 (over x, y).
Axes of the slice: x: 4, y: 4, z: 4, core: 2. Of those that a mesh axis runs over, the one named last changes fastest.
Arguments:
- ensemble: float32 [128, 512, 16, 128], P(None, 'mem', 'space'), may hold values from -6 to 6
- obs_cells: int32 [128, 2048], P(('mem', 'space')), may hold values from 0 to 2047
- obs_values: float32 [128, 2048], P(('mem', 'space')), may hold values from -6 to 6
- obs_rinv: float32 [128, 2048], P(('mem', 'space')), may hold values from 0.2 to 5
- obs_count: int32 [128], P(('mem', 'space')), may hold values from 512 to 2048
Outputs:
- analysis: float32 [128, 512, 16, 128], P(None, 'mem', 'space')
All inputs are finite; a program needn't handle non-finite values.
Results may differ from a plain program's by a relative error of at most 0.0003.
Values sent between devices are 32-bit elements; how exact they have to be, the bound alone decides.
No kernel may reach another device: no remote copies, remote signals or barrier semaphores. Data moves between devices by JAX's collectives and lax.ppermute only.
A program may use at most 128 MiB of HBM per device.

v0:
```python
import jax
import jax.numpy as jnp
from jax import lax
from jax.experimental import pallas as pl
from jax.experimental.pallas import tpu as pltpu
from jax.sharding import PartitionSpec as P

MEMBERS = 512
STEPS = 4
HALO = STEPS
LANES = 128
MESH = ("mem", "space")
RING = ("space", "mem")


NT = (((1,), (1,)), ((), ()))


def split(x):
    high = x.astype(jnp.bfloat16)
    return high, (x - high.astype(jnp.float32)).astype(jnp.bfloat16)


def dot(a, b, dims=(((1,), (0,)), ((), ()))):
    return lax.dot_general(a, b, dims, preferred_element_type=jnp.float32)


def dot3(a, b):
    return dot(a[0], b[0]) + (dot(a[0], b[1]) + dot(a[1], b[0]))


def obs_kernel(cells_ref, rinv_ref, values_ref, out_ref):
    cells = cells_ref[...]
    slots = cells.shape[1]
    strip = lax.broadcasted_iota(jnp.int32, (16, slots), 0) == (cells >> 7)
    lane = lax.broadcasted_iota(jnp.int32, (LANES, slots), 0) == (cells & 127)
    parts = []
    for value in (rinv_ref[...], rinv_ref[...] * values_ref[...]):
        for _ in range(3):
            part = value.astype(jnp.bfloat16).astype(jnp.float32)
            value = value - part
            parts.append(jnp.where(strip, part, 0.0).astype(jnp.bfloat16))
    total = dot(jnp.concatenate(parts, axis=0), lane.astype(jnp.float32).astype(jnp.bfloat16), NT)
    out_ref[0:16] = total[0:16] + total[16:32] + total[32:48]
    out_ref[16:32] = total[48:64] + total[64:80] + total[80:96]


def tiles_kernel(x_ref, u_ref, first_ref, last_ref):
    def strip(s, _):
        half = s // 8
        base = (s % 8) * 8
        for b in range(4):
            block = x_ref[pl.ds(s * 8 + 2 * b, 2)].reshape(LANES, LANES)
            turned = (block * 0.5).T
            for j in range(8):
                for g in range(2):
                    u_ref[base + j, pl.ds(64 * g + half * 4 + b, 8, stride=8), :] = turned[
                        j * 16 + 8 * g : j * 16 + 8 * g + 8
                    ]
        return 0

    lax.fori_loop(0, 16, strip, 0)

    def edge(r, _):
        first_ref[r] = u_ref[r, 0 : HALO * 8, :]
        last_ref[r] = u_ref[r, (16 - HALO) * 8 :, :]
        return 0

    lax.fori_loop(0, 64, edge, 0)


def sweep(load, store, columns, scale):
    width = len(columns)

    def row(r, n, c, s):
        west = load(r, columns[0] - 1)
        east = load(r, columns[-1] + 1)
        around = [west] + list(c) + [east]
        for i in range(width):
            p = around[i + 2] + s[i]
            q = around[i] + n[i]
            store(r, columns[i], scale * ((c[i] + (p + q)) - c[i] * (p - q)))

    def inner(r, carry):
        n, c = carry
        s = tuple(load(r + 1, k) for k in columns)
        row(r, n, c, s)
        return c, s

    n = tuple(pltpu.roll(load(63, k), 4, 0) for k in columns)
    c = tuple(load(0, k) for k in columns)
    wrapped = tuple(pltpu.roll(t, 4, 0) for t in c)
    n, c = lax.fori_loop(0, 63, inner, (n, c), unroll=3)
    row(63, n, c, wrapped)


def pieces(low, high, most):
    count = -(-(high - low) // most)
    edges = [low + (high - low) * i // count for i in range(count + 1)]
    return [list(range(a, b)) for a, b in zip(edges[:-1], edges[1:])]


def forecast(u_ref, west_ref, east_ref, a_ref, b_ref, f_ref):
    def at(col):
        return pl.ds(col * 8, 8)

    def start(r, col):
        if col < 0:
            return west_ref[r, at(col + HALO), :]
        if col >= 16:
            return east_ref[r, at(col - 16), :]
        return u_ref[r, at(col), :]

    def wide(ref):
        return lambda r, col: ref[r, at(col + HALO), :]

    def put(ref, shift):
        def store(r, col, value):
            ref[r, at(col + shift), :] = value

        return store

    loads = [start, wide(a_ref), wide(b_ref), wide(a_ref)]
    stores = [put(a_ref, HALO), put(b_ref, HALO), put(a_ref, HALO), put(f_ref, 0)]
    for step in range(STEPS):
        reach = HALO - 1 - step
        for columns in pieces(-reach, 16 + reach, 8):
            sweep(loads[step], stores[step], columns, 0.4 if step == STEPS - 1 else 0.2)


def analysis_kernel(
    u_ref, west_ref, east_ref, obs_ref, out_ref,
    a_ref, b_ref, f_ref, mean_ref, ah_ref, al_ref, bh_ref, bl_ref, proj_ref, t_ref, z_ref,
):
    forecast(u_ref, west_ref, east_ref, a_ref, b_ref, f_ref)
    proj_ref[...] = jnp.zeros_like(proj_ref)

    def strip(s, _):
        half = s // 8
        base = (s % 8) * 8
        blocks = []
        for b in range(4):
            rows = [
                f_ref[base + j, pl.ds(64 * g + half * 4 + b, 8, stride=8), :]
                for j in range(8)
                for g in range(2)
            ]
            blocks.append(jnp.concatenate(rows, axis=0).T)
        total = blocks[0] + blocks[1] + blocks[2] + blocks[3]
        mean = jnp.sum(total, axis=0, keepdims=True) * (1.0 / MEMBERS)
        mean_ref[pl.ds(s, 1)] = mean
        weight = obs_ref[pl.ds(s, 1)]
        root = jnp.sqrt(weight)
        misfit = obs_ref[pl.ds(s + 16, 1)] - weight * mean
        lanes = pl.ds(pl.multiple_of(s * LANES, LANES), LANES)
        for b in range(4):
            part = pl.ds(b * LANES, LANES)
            anomaly = blocks[b] - mean
            ah_ref[part, lanes], al_ref[part, lanes] = split(anomaly)
            bh_ref[part, lanes], bl_ref[part, lanes] = split(anomaly * root)
            proj_ref[part] += anomaly * misfit
        return 0

    lax.fori_loop(0, 16, strip, 0)

    shape = (MEMBERS, MEMBERS)
    diagonal = lax.broadcasted_iota(jnp.int32, shape, 0) == lax.broadcasted_iota(jnp.int32, shape, 1)

    def plus(coefficient, x):
        return x + jnp.where(diagonal, coefficient, 0.0)

    high, low = bh_ref[...], bl_ref[...]
    cross = dot(high, low, NT)
    matrix = plus(1.0, dot(high, high, NT) + (cross + dot(low, high, NT)))
    norm = jnp.sqrt(jnp.sum(jnp.sum(matrix * matrix, axis=0, keepdims=True), axis=1, keepdims=True))
    t_ref[...] = matrix * (1.0 / norm)

    for pair in range(3):
        t = t_ref[...]
        ts = split(t)
        square = dot3(ts, ts)
        inner = plus(1.6875, 0.0625 * square - 0.5625 * t)
        both = plus(2.25, dot3(split(square), split(inner)) - 2.4375 * t)
        us = split(both)
        if pair < 2:
            t_ref[...] = dot3(split(dot3(ts, us)), us)
        z_ref[...] = both if pair == 0 else dot3(us, split(z_ref[...]))

    root = z_ref[...] * (1.0 / jnp.sqrt(norm))
    projected = jnp.sum(proj_ref[...], axis=1, keepdims=True)
    once = jnp.sum(root * projected, axis=0, keepdims=True)
    once = jnp.broadcast_to(once, (8, MEMBERS)).T[:, 0:1]
    shift = jnp.sum(root * once, axis=0, keepdims=True)
    weights = split(root + shift)

    def columns(q, _):
        lanes = pl.ds(pl.multiple_of(q * 256, 256), 256)
        result = dot3(weights, (ah_ref[:, lanes], al_ref[:, lanes]))
        for i in range(2):
            piece = result[:, i * LANES : (i + 1) * LANES] + mean_ref[pl.ds(2 * q + i, 1)]
            out_ref[pl.ds((2 * q + i) * 8, 8)] = piece.reshape(8, 64, LANES)
        return 0

    lax.fori_loop(0, 8, columns, 0)


def vmem(count):
    return [pl.BlockSpec(memory_space=pltpu.VMEM) for _ in range(count)]


def f32(*shape):
    return jax.ShapeDtypeStruct(shape, jnp.float32)


def body(ensemble, obs_cells, obs_values, obs_rinv, obs_count):
    regions, block = ensemble.shape[0], ensemble.shape[1]
    params = pltpu.CompilerParams(vmem_limit_bytes=60 * 2**20)

    slots = lax.broadcasted_iota(jnp.int32, obs_cells.shape, 1)
    active = (slots < obs_count[:, None]).astype(jnp.float32)
    rinv = obs_rinv * active / (MEMBERS - 1.0)
    grids = pl.pallas_call(
        obs_kernel, out_shape=f32(32, LANES), in_specs=vmem(3), out_specs=vmem(1)[0],
        compiler_params=params, name="observations",
    )(obs_cells, rinv, obs_values)
    owner = [(r % 8) * 16 + r // 8 for r in range(regions)]
    grids = lax.ppermute(grids, MESH, list(enumerate(owner)))

    pieces_in = lax.all_to_all(
        ensemble.reshape(regions, block, LANES), RING, split_axis=0, concat_axis=0, tiled=True
    )
    tiles, first, last = pl.pallas_call(
        tiles_kernel,
        out_shape=[f32(64, 128, LANES), f32(64, HALO * 8, LANES), f32(64, HALO * 8, LANES)],
        in_specs=vmem(1), out_specs=vmem(3), compiler_params=params, name="tiles",
    )(pieces_in)
    after = [(owner[r], owner[(r + 1) % regions]) for r in range(regions)]
    before = [(owner[(r + 1) % regions], owner[r]) for r in range(regions)]
    west = lax.ppermute(last, MESH, after)
    east = lax.ppermute(first, MESH, before)
    half = pltpu.VMEM((MEMBERS, 2048), jnp.bfloat16)
    square = pltpu.VMEM((MEMBERS, MEMBERS), jnp.float32)
    wide = pltpu.VMEM((64, (16 + 2 * HALO) * 8, LANES), jnp.float32)
    analysed = pl.pallas_call(
        analysis_kernel,
        out_shape=f32(regions, block, LANES),
        in_specs=vmem(4), out_specs=vmem(1)[0],
        scratch_shapes=[
            wide, wide, pltpu.VMEM((64, 128, LANES), jnp.float32), pltpu.VMEM((16, LANES), jnp.float32),
            half, half, half, half, pltpu.VMEM((MEMBERS, LANES), jnp.float32), square, square,
        ],
        compiler_params=params, name="analysis",
    )(tiles, west, east, grids)
    returned = lax.all_to_all(analysed, RING, split_axis=0, concat_axis=0, tiled=True)
    return returned.reshape(ensemble.shape)


def solution(mesh):
    return jax.shard_map(
        body,
        mesh=mesh,
        in_specs=(
            P(None, "mem", "space", None),
            P(("mem", "space"), None),
            P(("mem", "space"), None),
            P(("mem", "space"), None),
            P(("mem", "space")),
        ),
        out_specs=P(None, "mem", "space", None),
        check_vma=False,
    )
```

profile of v0, /device:TPU:1, one launch (start us, length us, event | category | flops | bytes accessed | tf_op | source)
XLA Modules:
  0.0 192.9 jit_solution(14208276539375674024)
XLA Ops:
  0.0 64.7 %all_to_all.10.x_ref = f32[128,64,128]{2,1,0:T(8,128)} all-to-all(f32[128,64,128]{2,1,0:T(8,128)} %bitcast.7), channel_id=1, replica_groups=mesh['mem'=8,'space'=16] {'space','mem'}, dimensions={0} | all-to-all | bytes 8388608 | tf_op jit(solution)/shard_map/all_to_all | solution.py:229
  64.7 0.0 copy-start.3
  64.7 7.5 %tiles.1 = (f32[64,128,128]{2,1,0:T(8,128)}, f32[64,32,128]{2,1,0:T(8,128)}, f32[64,32,128]{2,1,0:T(8,128)}) custom-call(f32[128,64,128]{2,1,0:T(8,128)} %all_to_all.10.x_ref), custom_call_target="tpu_custom_call" | custom-call | tf_op jit(solution)/shard_map/tiles/pallas_call | solution.py:232
  72.2 1.0 collective-permute-start
  73.2 0.1 collective-permute-start.1
  74.0 0.0 copy-done.3
  74.0 0.6 fusion.rinv_ref
  74.6 1.6 observations.1
  76.3 5.5 %collective-permute-start.2 = (f32[32,128]{1,0:T(8,128)}, f32[32,128]{1,0:T(8,128)S(1)}, u32[]{:S(2)}, u32[]{:S(2)}) collective-permute-start(f32[32,128]{1,0:T(8,128)} %observations.1), channel_id=1, source_target_pairs={{0,0},{1,16},{2,32},{3,48},{4,64},{5,80},{6,96},{7,112},{8,1},{9,1... | collective-permute-start | bytes 49160 | tf_op jit(solution)/shard_map/ppermute | solution.py:227
  81.8 9.2 %collective-permute-done.2.obs_ref = f32[32,128]{1,0:T(8,128)S(1)} collective-permute-done((f32[32,128]{1,0:T(8,128)}, f32[32,128]{1,0:T(8,128)S(1)}, u32[]{:S(2)}, u32[]{:S(2)}) %collective-permute-start.2) | collective-permute-done | bytes 16416 | tf_op jit(solution)/shard_map/ppermute | solution.py:227
  91.0 0.0 copy-start.2
  91.0 0.0 collective-permute-done.west_ref
  91.0 0.0 copy-start
  91.0 0.0 collective-permute-done.1.east_ref
  91.0 0.0 copy-start.1
  91.0 0.6 copy-done.2
  91.6 0.4 copy-done
  92.0 0.3 copy-done.1
  92.3 35.7 %analysis.1 = f32[128,64,128]{2,1,0:T(8,128)} custom-call(f32[64,128,128]{2,1,0:T(8,128)} %get-tuple-element.8.u_ref, f32[64,32,128]{2,1,0:T(8,128)} %copy-done, f32[64,32,128]{2,1,0:T(8,128)} %copy-done.1, f32[32,128]{1,0:T(8,128)} %copy-done.2), custom_call_target="tpu_custom_call" | custom-call | tf_op jit(solution)/shard_map/analysis/pallas_call | solution.py:244
  128.0 63.0 %all_to_all.11 = f32[128,64,128]{2,1,0:T(8,128)S(1)} all-to-all(f32[128,64,128]{2,1,0:T(8,128)} %analysis.1), channel_id=1, replica_groups=mesh['mem'=8,'space'=16] {'space','mem'}, dimensions={0} | all-to-all | bytes 8388608 | tf_op jit(solution)/shard_map/all_to_all | solution.py:254
  190.9 2.0 %copy.9 = f32[128,64,1,128]{3,2,1,0:T(1,128)} copy(f32[128,64,1,128]{3,2,1,0:T(1,128)S(1)} %bitcast.6) | data formatting | bytes 8388608
Async XLA Ops:
  64.7 9.3 %copy-start.3 = (f32[1,2048]{1,0:T(1,128)S(1)}, f32[1,2048]{1,0:T(1,128)}, u32[]{:S(2)}) copy-start(f32[1,2048]{1,0:T(1,128)} %param.8) | copy-start | bytes 24580
  72.2 18.8 %collective-permute-start = (f32[64,32,128]{2,1,0:T(8,128)}, f32[64,32,128]{2,1,0:T(8,128)S(1)}, u32[]{:S(2)}, u32[]{:S(2)}) collective-permute-start(f32[64,32,128]{2,1,0:T(8,128)} %get-tuple-element.9), channel_id=1, source_target_pairs={{0,16},{16,32},{32,48},{48,64},{64,80},{80,96},{96,112},{112,1},{1... | collective-permute-start | bytes 3145736 | tf_op jit(solution)/shard_map/ppermute | solution.py:239
  73.2 17.8 %collective-permute-start.1 = (f32[64,32,128]{2,1,0:T(8,128)}, f32[64,32,128]{2,1,0:T(8,128)S(1)}, u32[]{:S(2)}, u32[]{:S(2)}) collective-permute-start(f32[64,32,128]{2,1,0:T(8,128)} %get-tuple-element.10), channel_id=1, source_target_pairs={{16,0},{32,16},{48,32},{64,48},{80,64},{96,80},{112,96},{1,112},{1... | collective-permute-start | bytes 3145736 | tf_op jit(solution)/shard_map/ppermute | solution.py:240
  76.3 14.7 %collective-permute-start.2 = (f32[32,128]{1,0:T(8,128)}, f32[32,128]{1,0:T(8,128)S(1)}, u32[]{:S(2)}, u32[]{:S(2)}) collective-permute-start(f32[32,128]{1,0:T(8,128)} %observations.1), channel_id=1, source_target_pairs={{0,0},{1,16},{2,32},{3,48},{4,64},{5,80},{6,96},{7,112},{8,1},{9,1... | collective-permute-start | bytes 49160 | tf_op jit(solution)/shard_map/ppermute | solution.py:227
  91.0 0.6 copy-start.2
  91.0 1.0 copy-start
  91.0 1.3 copy-start.1
where the time goes:
time: 193 us
  blocking collectives  128 us (66%)
  Pallas kernels  44.9 us (23%)
  waiting for transfers between devices  9.21 us (5%)
  starting transfers between devices  6.66 us (3%)
  local copies, waits for them, and re-layouts  3.3 us (2%)
    all_to_all x1, blocking collectives, body(): lax.all_to_all(ensemble.reshape(regions, block, LANES), RING, split_axis=...  64.7 us
    all_to_all x1, blocking collectives, body(): lax.all_to_all(analysed, RING, split_axis=0, concat_axis=0, tiled=True)  63 us
    pallas_call x1, Pallas kernels, body(): pl.pallas_call(analysis_kernel, out_shape=f32(regions, block, LANES), in_...  35.7 us
    ppermute x1, waiting for transfers between devices, body(): grids = lax.ppermute(grids, MESH, list(enumerate(owner)))  9.21 us
    pallas_call x1, Pallas kernels, body(): pl.pallas_call(tiles_kernel, out_shape=[f32(64, 128, LANES), f32(64, HALO...  7.53 us
    ppermute x1, starting transfers between devices, body(): grids = lax.ppermute(grids, MESH, list(enumerate(owner)))  5.52 us
  transfers between devices with their start and end apart: 3, of which 1 were waited for; matrix products, arithmetic and copies ran while one was open for 0% of the time, Pallas kernels for 1%

commit v1 on v0

v1 whole, which is shorter than its diff:
```python
import jax
import jax.numpy as jnp
from jax import lax
from jax.experimental import pallas as pl
from jax.experimental.pallas import tpu as pltpu
from jax.sharding import PartitionSpec as P

MEMBERS = 512
STEPS = 4
HALO = STEPS
LANES = 128
MESH = ("mem", "space")
RING = ("space", "mem")


NT = (((1,), (1,)), ((), ()))


def split(x):
    high = x.astype(jnp.bfloat16)
    return high, (x - high.astype(jnp.float32)).astype(jnp.bfloat16)


def dot(a, b, dims=(((1,), (0,)), ((), ()))):
    return lax.dot_general(a, b, dims, preferred_element_type=jnp.float32)


def dot3(a, b):
    return dot(a[0], b[0]) + (dot(a[0], b[1]) + dot(a[1], b[0]))


def obs_kernel(cells_ref, rinv_ref, values_ref, out_ref):
    cells = cells_ref[...]
    slots = cells.shape[1]
    row, col = cells >> 4, cells & 15
    outer = ((col + 4) & 15) < 8
    place = (row >> 4) + jnp.where(outer, 8, 0)
    group = lax.broadcasted_iota(jnp.int32, (16, slots), 0) == place
    lane = lax.broadcasted_iota(jnp.int32, (LANES, slots), 0) == (row & 15) * 8 + (col & 7)
    parts = []
    for value in (rinv_ref[...], rinv_ref[...] * values_ref[...]):
        for _ in range(3):
            part = value.astype(jnp.bfloat16).astype(jnp.float32)
            value = value - part
            parts.append(jnp.where(group, part, 0.0).astype(jnp.bfloat16))
    total = dot(jnp.concatenate(parts, axis=0), lane.astype(jnp.float32).astype(jnp.bfloat16), NT)
    out_ref[0:16] = total[0:16] + total[16:32] + total[32:48]
    out_ref[16:32] = total[48:64] + total[64:80] + total[80:96]


def at(col):
    return pl.ds(col * 8, 8)


def tiles_kernel(x_ref, u_ref, first_ref, last_ref):
    def strip(s, _):
        half = s // 8
        base = (s % 8) * 8
        for b in range(4):
            block = x_ref[pl.ds(s * 8 + 2 * b, 2)].reshape(LANES, LANES)
            turned = (block * 0.5).T
            for j in range(8):
                for g in range(2):
                    u_ref[base + j, pl.ds(64 * g + half * 4 + b, 8, stride=8), :] = turned[
                        j * 16 + 8 * g : j * 16 + 8 * g + 8
                    ]
        return 0

    lax.fori_loop(0, 16, strip, 0)

    def edge(r, _):
        first_ref[r] = u_ref[r, 0 : HALO * 8, :]
        last_ref[r] = u_ref[r, (16 - HALO) * 8 :, :]
        return 0

    lax.fori_loop(0, 64, edge, 0, unroll=4)


def sweep(load, store, columns, scale):
    width = len(columns)

    def row(r, n, c, s):
        west = load(r, columns[0] - 1)
        east = load(r, columns[-1] + 1)
        around = [west] + list(c) + [east]
        for i in range(width):
            p = around[i + 2] + s[i]
            q = around[i] + n[i]
            store(r, columns[i], scale * ((c[i] + (p + q)) - c[i] * (p - q)))

    def body(r, carry):
        n, c = carry
        s = tuple(load(r + 1, k) for k in columns)
        row(r, n, c, s)
        return c, s

    n = tuple(pltpu.roll(load(63, k), 4, 0) for k in columns)
    c = tuple(load(0, k) for k in columns)
    wrapped = tuple(pltpu.roll(t, 4, 0) for t in c)
    n, c = lax.fori_loop(0, 63, body, (n, c), unroll=3)
    row(63, n, c, wrapped)


def pieces(low, high, most):
    count = -(-(high - low) // most)
    edges = [low + (high - low) * i // count for i in range(count + 1)]
    return [list(range(a, b)) for a, b in zip(edges[:-1], edges[1:])]


def scale_of(step):
    return 0.4 if step == STEPS - 1 else 0.2


def inner_kernel(u_ref, one_ref, two_ref, three_ref, inner_ref):
    levels = [u_ref, one_ref, two_ref, three_ref]
    for step in range(STEPS):
        low, high = step + 1, 15 - step

        def load(r, col, step=step):
            return levels[step][r, at(col - step), :]

        def store(r, col, value, step=step, low=low):
            if step < STEPS - 1:
                levels[step + 1][r, at(col - low), :] = value
            else:
                inner_ref[r, at(col & 7), :] = value

        for columns in pieces(low, high, 8):
            sweep(load, store, columns, scale_of(step))


def outer_forecast(levels, west_ref, east_ref, wests, easts, outer_ref):
    for step in range(STEPS):
        reach = HALO - step

        def load(r, col, step=step, reach=reach):
            if step == 0:
                if col < 0:
                    return west_ref[r, at(col + HALO), :]
                if col >= 16:
                    return east_ref[r, at(col - 16), :]
            elif col < step:
                return wests[step - 1][r, at(col + reach), :]
            elif col >= 16 - step:
                return easts[step - 1][r, at(col - 16 + step), :]
            return levels[step][r, at(col - step), :]

        def store(r, col, value, step=step, reach=reach):
            if step == STEPS - 1:
                outer_ref[r, at(col & 7), :] = value
            elif col < 8:
                wests[step][r, at(col + reach - 1), :] = value
            else:
                easts[step][r, at(col - 15 + step), :] = value

        sweep(load, store, list(range(1 - reach, step + 1)), scale_of(step))
        sweep(load, store, list(range(15 - step, 15 + reach)), scale_of(step))


def turned_rows(load, half, b, count):
    return jnp.concatenate([load(j, half * 4 + b) for j in range(count)], axis=0).T


def place_of(sub):
    return pl.ds(sub, 8, stride=8)


def gather_groups(part_ref, obs_ref, first_group, bh_ref, bl_ref, proj_ref):
    def group(q, _):
        half = q // 4
        base = (q % 4) * 16
        blocks = [
            turned_rows(lambda j, sub: part_ref[base + j, place_of(sub), :], half, b, 16)
            for b in range(4)
        ]
        total = blocks[0] + blocks[1] + blocks[2] + blocks[3]
        mean = jnp.sum(total, axis=0, keepdims=True) * (1.0 / MEMBERS)
        weight = obs_ref[pl.ds(first_group + q, 1)]
        root = jnp.sqrt(weight)
        misfit = obs_ref[pl.ds(first_group + q + 16, 1)] - weight * mean
        lanes = pl.ds(pl.multiple_of(q * LANES, LANES), LANES)
        for b in range(4):
            part = pl.ds(b * LANES, LANES)
            anomaly = blocks[b] - mean
            bh_ref[part, lanes], bl_ref[part, lanes] = split(anomaly * root)
            proj_ref[part] += anomaly * misfit
        return 0

    lax.fori_loop(0, 8, group, 0)
    high, low = bh_ref[...], bl_ref[...]
    return dot(high, high, NT) + (dot(high, low, NT) + dot(low, high, NT))


def inner_sums_kernel(inner_ref, obs_ref, matrix_ref, proj_ref, bh_ref, bl_ref):
    proj_ref[...] = jnp.zeros_like(proj_ref)
    matrix_ref[...] = gather_groups(inner_ref, obs_ref, 0, bh_ref, bl_ref, proj_ref)


def analysis_kernel(
    u_ref, one_ref, two_ref, three_ref, inner_ref, west_ref, east_ref, obs_ref, matrix_ref, sums_ref,
    out_ref,
    w1_ref, w2_ref, w3_ref, e1_ref, e2_ref, e3_ref, outer_ref,
    mean_ref, ah_ref, al_ref, bh_ref, bl_ref, proj_ref, t_ref, z_ref,
):
    outer_forecast(
        [u_ref, one_ref, two_ref, three_ref], west_ref, east_ref,
        [w1_ref, w2_ref, w3_ref], [e1_ref, e2_ref, e3_ref], outer_ref,
    )
    proj_ref[...] = sums_ref[...]
    matrix = matrix_ref[...] + gather_groups(outer_ref, obs_ref, 8, bh_ref, bl_ref, proj_ref)
    t_ref[...] = matrix

    low_half = lax.broadcasted_iota(jnp.int32, (8, LANES), 0) < 4

    def strip(s, _):
        half = s // 8
        base = (s % 8) * 8
        blocks = []
        for b in range(4):
            rows = []
            for j in range(8):
                sub = place_of(half * 4 + b)
                near = inner_ref[base + j, sub, :]
                far = outer_ref[base + j, sub, :]
                rows += [jnp.where(low_half, far, near), jnp.where(low_half, near, far)]
            blocks.append(jnp.concatenate(rows, axis=0).T)
        total = blocks[0] + blocks[1] + blocks[2] + blocks[3]
        mean = jnp.sum(total, axis=0, keepdims=True) * (1.0 / MEMBERS)
        mean_ref[pl.ds(s, 1)] = mean
        lanes = pl.ds(pl.multiple_of(s * LANES, LANES), LANES)
        for b in range(4):
            part = pl.ds(b * LANES, LANES)
            ah_ref[part, lanes], al_ref[part, lanes] = split(blocks[b] - mean)
        return 0

    lax.fori_loop(0, 16, strip, 0)

    shape = (MEMBERS, MEMBERS)
    diagonal = lax.broadcasted_iota(jnp.int32, shape, 0) == lax.broadcasted_iota(jnp.int32, shape, 1)

    def plus(coefficient, x):
        return x + jnp.where(diagonal, coefficient, 0.0)

    matrix = plus(1.0, t_ref[...])
    norm = jnp.sqrt(jnp.sum(jnp.sum(matrix * matrix, axis=0, keepdims=True), axis=1, keepdims=True))
    t_ref[...] = matrix * (1.0 / norm)

    for pair in range(3):
        t = t_ref[...]
        ts = split(t)
        square = dot3(ts, ts)
        inner = plus(1.6875, 0.0625 * square - 0.5625 * t)
        both = plus(2.25, dot3(split(square), split(inner)) - 2.4375 * t)
        us = split(both)
        if pair < 2:
            t_ref[...] = dot3(split(dot3(ts, us)), us)
        z_ref[...] = both if pair == 0 else dot3(us, split(z_ref[...]))

    root = z_ref[...] * (1.0 / jnp.sqrt(norm))
    projected = jnp.sum(proj_ref[...], axis=1, keepdims=True)
    once = jnp.sum(root * projected, axis=0, keepdims=True)
    once = jnp.broadcast_to(once, (8, MEMBERS)).T[:, 0:1]
    shift = jnp.sum(root * once, axis=0, keepdims=True)
    weights = split(root + shift)

    def result_of(q, _):
        lanes = pl.ds(pl.multiple_of(q * 256, 256), 256)
        result = dot3(weights, (ah_ref[:, lanes], al_ref[:, lanes]))
        for i in range(2):
            piece = result[:, i * LANES : (i + 1) * LANES] + mean_ref[pl.ds(2 * q + i, 1)]
            out_ref[pl.ds((2 * q + i) * 8, 8)] = piece.reshape(8, 64, LANES)
        return 0

    lax.fori_loop(0, 8, result_of, 0)


def vmem(count):
    return [pl.BlockSpec(memory_space=pltpu.VMEM) for _ in range(count)]


def call(kernel, outs, scratch, limit, flops, name, *operands):
    operands = [pltpu.with_memory_space_constraint(x, pltpu.VMEM) for x in operands]
    return pl.pallas_call(
        kernel,
        out_shape=[pltpu.VMEM(shape, jnp.float32) for shape in outs],
        in_specs=vmem(len(operands)),
        out_specs=vmem(len(outs)),
        scratch_shapes=[pltpu.VMEM(*shape) for shape in scratch],
        compiler_params=pltpu.CompilerParams(vmem_limit_bytes=limit * 2**20),
        cost_estimate=pl.CostEstimate(flops=flops, transcendentals=0, bytes_accessed=2**20),
        name=name,
    )(*operands)


def columns(count):
    return (64, count * 8, LANES)


def body(ensemble, obs_cells, obs_values, obs_rinv, obs_count):
    regions, block = ensemble.shape[0], ensemble.shape[1]
    owner = [(r % 8) * 16 + r // 8 for r in range(regions)]
    after = [(owner[r], owner[(r + 1) % regions]) for r in range(regions)]
    before = [(owner[(r + 1) % regions], owner[r]) for r in range(regions)]
    unit = 10**9

    slots = lax.broadcasted_iota(jnp.int32, obs_cells.shape, 1)
    active = (slots < obs_count[:, None]).astype(jnp.float32)
    rinv = obs_rinv * active / (MEMBERS - 1.0)
    grids = pl.pallas_call(
        obs_kernel, out_shape=pltpu.VMEM((32, LANES), jnp.float32), in_specs=vmem(3), out_specs=vmem(1)[0],
        compiler_params=pltpu.CompilerParams(vmem_limit_bytes=4 * 2**20), name="observations",
    )(obs_cells, rinv, obs_values)
    grids = lax.ppermute(grids, MESH, list(enumerate(owner)))
    pieces_in = lax.all_to_all(
        ensemble.reshape(regions, block, LANES), RING, split_axis=0, concat_axis=0, tiled=True
    )
    pieces_in, grids = lax.optimization_barrier((pieces_in, grids))
    tiles, first, last = call(
        tiles_kernel, [columns(16), columns(HALO), columns(HALO)], [], 8, unit, "tiles", pieces_in
    )
    west = lax.ppermute(last, MESH, after)
    east = lax.ppermute(first, MESH, before)
    levels = call(
        inner_kernel, [columns(14), columns(12), columns(10), columns(8)], [], 2, 4 * unit, "inner", tiles
    )

    f32, bf16 = jnp.float32, jnp.bfloat16
    half = ((MEMBERS, 1024), bf16)
    whole = ((MEMBERS, 2048), bf16)
    square = ((MEMBERS, MEMBERS), f32)
    sums = (MEMBERS, LANES)
    matrix, projected = call(
        inner_sums_kernel, [square[0], sums], [half, half], 8, 6 * unit, "inner_sums", levels[3], grids
    )
    side = (columns(HALO), f32)
    (analysed,) = call(
        analysis_kernel,
        [(regions, block, LANES)],
        [side] * 6
        + [(columns(8), f32), ((16, LANES), f32), whole, whole, half, half, (sums, f32), square, square],
        24, 30 * unit, "analysis", tiles, *levels, west, east, grids, matrix, projected,
    )
    returned = lax.all_to_all(analysed, RING, split_axis=0, concat_axis=0, tiled=True)
    return returned.reshape(ensemble.shape)


def solution(mesh):
    return jax.shard_map(
        body,
        mesh=mesh,
        in_specs=(
            P(None, "mem", "space", None),
            P(("mem", "space"), None),
            P(("mem", "space"), None),
            P(("mem", "space"), None),
            P(("mem", "space")),
        ),
        out_specs=P(None, "mem", "space", None),
        check_vma=False,
    )
```

time: 193 us -> 180 us (0.933)
  blocking collectives: 128 us -> 66.3 us
  waiting for transfers between devices: 9.21 us -> 53.1 us
  starting transfers between devices: 6.66 us -> 18.4 us
  Pallas kernels: 44.9 us -> 39.3 us
    all_to_all x1 -> x0, blocking collectives: 64.7 us -> none  [body(): lax.all_to_all(ensemble.reshape(regions, block, LANES), RING, split_axis=...]
    ppermute x1, waiting for transfers between devices: 9.21 us -> 33.6 us  [body(): grids = lax.ppermute(grids, MESH, list(enumerate(owner)))]
    all_to_all x0 -> x1, waiting for transfers between devices: none -> 13.1 us  [body(): lax.all_to_all(ensemble.reshape(regions, block, LANES), RING, split_axis=...]
    all_to_all x0 -> x1, starting transfers between devices: none -> 12 us  [body(): lax.all_to_all(ensemble.reshape(regions, block, LANES), RING, split_axis=...]
    pallas_call x3 -> x5, Pallas kernels: 44.9 us -> 39.3 us  [the longest x4 39 us: call(): pl.pallas_call(kernel, out_shape=[pltpu.VMEM(shape, jnp.float32) for shap...]
    ppermute x1, waiting for transfers between devices: 0.01 us -> 3.69 us  [body(): west = lax.ppermute(last, MESH, after)]
    all_to_all x1, blocking collectives: 63 us -> 66.3 us  [body(): lax.all_to_all(analysed, RING, split_axis=0, concat_axis=0, tiled=True)]
    ppermute x1, waiting for transfers between devices: 0.01 us -> 2.77 us  [body(): east = lax.ppermute(first, MESH, before)]
  transfers between devices with their start and end apart: 3 -> 4, of which waited for: 1 -> 4; matrix products, arithmetic and copies ran while one was open for 0% -> 0% of each run, Pallas kernels for 1% -> 4%
where the time goes in v1:
time: 180 us
  blocking collectives  66.3 us (37%)
  waiting for transfers between devices  53.1 us (30%)
  Pallas kernels  39.3 us (22%)
  starting transfers between devices  18.4 us (10%)
  local copies, waits for them, and re-layouts  2.02 us (1%)
    all_to_all x1, blocking collectives, body(): lax.all_to_all(analysed, RING, split_axis=0, concat_axis=0, tiled=True)  66.3 us
    pallas_call x4, Pallas kernels, call(): pl.pallas_call(kernel, out_shape=[pltpu.VMEM(shape, jnp.float32) for shap...  39 us
    ppermute x1, waiting for transfers between devices, body(): grids = lax.ppermute(grids, MESH, list(enumerate(owner)))  33.6 us
    all_to_all x1, waiting for transfers between devices, body(): lax.all_to_all(ensemble.reshape(regions, block, LANES), RING, split_axis=...  13.1 us
    all_to_all x1, starting transfers between devices, body(): lax.all_to_all(ensemble.reshape(regions, block, LANES), RING, split_axis=...  12 us
    ppermute x1, starting transfers between devices, body(): grids = lax.ppermute(grids, MESH, list(enumerate(owner)))  5.06 us
    ppermute x1, waiting for transfers between devices, body(): west = lax.ppermute(last, MESH, after)  3.69 us
  transfers between devices with their start and end apart: 4, of which 4 were waited for; matrix products, arithmetic and copies ran while one was open for 0% of the time, Pallas kernels for 4%

profile of v1, /device:TPU:1, one launch (start us, length us, event | category | flops | bytes accessed | tf_op | source)
XLA Modules:
  0.0 179.9 jit_solution(8621353336649960574)
XLA Ops:
  0.0 0.0 copy-start.2
  0.0 0.0 copy-start
  0.0 0.0 copy-start.1
  0.0 12.0 %all-to-all-start = ((f32[128,64,128]{2,1,0:T(8,128)}), f32[128,64,128]{2,1,0:T(8,128)}, u32[]{:S(2)}, u32[]{:S(2)}) async-start(f32[128,64,128]{2,1,0:T(8,128)} %bitcast.7), calls=%async_computation | async-start | bytes 8388608 | tf_op jit(solution)/shard_map/all_to_all | solution.py:314
  12.6 0.0 copy-done.2
  12.6 0.0 copy-done
  12.7 0.0 copy-done.1
  12.7 0.3 observations.1
  13.0 5.1 %collective-permute-start = (f32[32,128]{1,0:T(8,128)S(1)}, f32[32,128]{1,0:T(8,128)S(1)}, u32[]{:S(2)}, u32[]{:S(2)}) collective-permute-start(f32[32,128]{1,0:T(8,128)S(1)} %observations.1), channel_id=1, source_target_pairs={{0,0},{1,16},{2,32},{3,48},{4,64},{5,80},{6,96},{7,112},{8,1},{9,1... | collective-permute-start | bytes 49160 | tf_op jit(solution)/shard_map/ppermute | solution.py:313
  18.0 33.6 %collective-permute-done.obs_ref = f32[32,128]{1,0:T(8,128)S(1)} collective-permute-done((f32[32,128]{1,0:T(8,128)S(1)}, f32[32,128]{1,0:T(8,128)S(1)}, u32[]{:S(2)}, u32[]{:S(2)}) %collective-permute-start) | collective-permute-done | bytes 16416 | tf_op jit(solution)/shard_map/ppermute | solution.py:313
  51.6 13.1 %all-to-all-done.x_ref = f32[128,64,128]{2,1,0:T(8,128)} async-done(((f32[128,64,128]{2,1,0:T(8,128)}), f32[128,64,128]{2,1,0:T(8,128)}, u32[]{:S(2)}, u32[]{:S(2)}) %all-to-all-start) | async-done | bytes 4194336 | tf_op jit(solution)/shard_map/all_to_all | solution.py:314
  64.7 4.5 %tiles.1 = (f32[64,128,128]{2,1,0:T(8,128)S(1)}, f32[64,32,128]{2,1,0:T(8,128)S(1)}, f32[64,32,128]{2,1,0:T(8,128)S(1)}) custom-call(f32[128,64,128]{2,1,0:T(8,128)} %all-to-all-done.x_ref), custom_call_target="tpu_custom_call" | custom-call | flops 1000000000 | bytes 1048576 | tf_op jit(solution)/shard_map/tiles/pallas_call | solution.py:283
  69.2 1.0 collective-permute-start.1
  70.2 0.4 collective-permute-start.2
  70.6 3.7 %inner.1 = (f32[64,112,128]{2,1,0:T(8,128)S(1)}, f32[64,96,128]{2,1,0:T(8,128)S(1)}, f32[64,80,128]{2,1,0:T(8,128)S(1)}, f32[64,64,128]{2,1,0:T(8,128)S(1)}) custom-call(f32[64,128,128]{2,1,0:T(8,128)S(1)} %get-tuple-element.17.u_ref), custom_call_target="tpu_custom_call" | custom-call | flops 4000000000 | bytes 1048576 | tf_op jit(solution)/shard_map/inner/pallas_call | solution.py:283
  74.3 4.0 %inner_sums.1 = (f32[512,512]{1,0:T(8,128)S(1)}, f32[512,128]{1,0:T(8,128)S(1)}) custom-call(f32[64,64,128]{2,1,0:T(8,128)S(1)} %get-tuple-element.21.inner_ref, f32[32,128]{1,0:T(8,128)S(1)} %collective-permute-done.obs_ref), custom_call_target="tpu_custom_call" | custom-call | flops 6000000000 | bytes 1048576 | tf_op jit(solution)/shard_map/inner_sums/pallas_call | solution.py:283
  78.3 3.7 %collective-permute-done.1.west_ref = f32[64,32,128]{2,1,0:T(8,128)S(1)} collective-permute-done((f32[64,32,128]{2,1,0:T(8,128)S(1)}, f32[64,32,128]{2,1,0:T(8,128)S(1)}, u32[]{:S(2)}, u32[]{:S(2)}) %collective-permute-start.1) | collective-permute-done | bytes 1048608 | tf_op jit(solution)/shard_map/ppermute | solution.py:321
  82.0 2.8 %collective-permute-done.2.east_ref = f32[64,32,128]{2,1,0:T(8,128)S(1)} collective-permute-done((f32[64,32,128]{2,1,0:T(8,128)S(1)}, f32[64,32,128]{2,1,0:T(8,128)S(1)}, u32[]{:S(2)}, u32[]{:S(2)}) %collective-permute-start.2) | collective-permute-done | bytes 1048608 | tf_op jit(solution)/shard_map/ppermute | solution.py:322
  84.8 26.8 %analysis.1 = f32[128,64,128]{2,1,0:T(8,128)S(1)} custom-call(f32[64,128,128]{2,1,0:T(8,128)S(1)} %get-tuple-element.17.u_ref, f32[64,112,128]{2,1,0:T(8,128)S(1)} %get-tuple-element.18.one_ref, f32[64,96,128]{2,1,0:T(8,128)S(1)} %get-tuple-element.19.two_ref, f32[64,80,128]{2,1,0:T(8,128)S(1)} %get-tuple-element.20.three_ref, ...), custom_call_target="tpu_custom_call" | custom-call | flops 30000001024 | bytes 1048576 | tf_op jit(solution)/shard_map/analysis/pallas_call | solution.py:283
  111.5 66.3 %all_to_all.10 = f32[128,64,128]{2,1,0:T(8,128)S(1)} all-to-all(f32[128,64,128]{2,1,0:T(8,128)S(1)} %analysis.1), channel_id=1, replica_groups=mesh['mem'=8,'space'=16] {'space','mem'}, dimensions={0} | all-to-all | bytes 8388608 | tf_op jit(solution)/shard_map/all_to_all | solution.py:343
  177.8 2.0 %copy.9 = f32[128,64,1,128]{3,2,1,0:T(1,128)} copy(f32[128,64,1,128]{3,2,1,0:T(1,128)S(1)} %bitcast.6) | data formatting | bytes 8388608
  (1 shorter events, 0.0 us)
Async XLA Ops:
  0.0 12.6 %copy-start.2 = (f32[1,2048]{1,0:T(1,128)S(1)}, f32[1,2048]{1,0:T(1,128)}, u32[]{:S(2)}) copy-start(f32[1,2048]{1,0:T(1,128)} %param.8) | copy-start | bytes 24580
  0.0 12.6 %copy-start = (s32[1,2048]{1,0:T(1,128)S(1)}, s32[1,2048]{1,0:T(1,128)}, u32[]{:S(2)}) copy-start(s32[1,2048]{1,0:T(1,128)} %cells_ref.1) | copy-start | bytes 24580
  0.0 12.7 %copy-start.1 = (f32[1,2048]{1,0:T(1,128)S(1)}, f32[1,2048]{1,0:T(1,128)}, u32[]{:S(2)}) copy-start(f32[1,2048]{1,0:T(1,128)} %values_ref.1) | copy-start | bytes 24580
  0.0 64.7 %all-to-all-start = ((f32[128,64,128]{2,1,0:T(8,128)}), f32[128,64,128]{2,1,0:T(8,128)}, u32[]{:S(2)}, u32[]{:S(2)}) async-start(f32[128,64,128]{2,1,0:T(8,128)} %bitcast.7), calls=%async_computation | async-start | bytes 8388608 | tf_op jit(solution)/shard_map/all_to_all | solution.py:314
  13.0 38.6 %collective-permute-start = (f32[32,128]{1,0:T(8,128)S(1)}, f32[32,128]{1,0:T(8,128)S(1)}, u32[]{:S(2)}, u32[]{:S(2)}) collective-permute-start(f32[32,128]{1,0:T(8,128)S(1)} %observations.1), channel_id=1, source_target_pairs={{0,0},{1,16},{2,32},{3,48},{4,64},{5,80},{6,96},{7,112},{8,1},{9,1... | collective-permute-start | bytes 49160 | tf_op jit(solution)/shard_map/ppermute | solution.py:313
  69.2 12.8 %collective-permute-start.1 = (f32[64,32,128]{2,1,0:T(8,128)S(1)}, f32[64,32,128]{2,1,0:T(8,128)S(1)}, u32[]{:S(2)}, u32[]{:S(2)}) collective-permute-start(f32[64,32,128]{2,1,0:T(8,128)S(1)} %get-tuple-element.22), channel_id=1, source_target_pairs={{0,16},{16,32},{32,48},{48,64},{64,80},{80,96},{96,112},{112,1},{1... | collective-permute-start | bytes 3145736 | tf_op jit(solution)/shard_map/ppermute | solution.py:321
  70.2 14.5 %collective-permute-start.2 = (f32[64,32,128]{2,1,0:T(8,128)S(1)}, f32[64,32,128]{2,1,0:T(8,128)S(1)}, u32[]{:S(2)}, u32[]{:S(2)}) collective-permute-start(f32[64,32,128]{2,1,0:T(8,128)S(1)} %get-tuple-element.23), channel_id=1, source_target_pairs={{16,0},{32,16},{48,32},{64,48},{80,64},{96,80},{112,96},{1,112},{1... | collective-permute-start | bytes 3145736 | tf_op jit(solution)/shard_map/ppermute | solution.py:322

commit v2 on v1

--- a/solution.py
+++ b/solution.py
@@ -36,7 +36,7 @@
     outer = ((col + 4) & 15) < 8
     place = (row >> 4) + jnp.where(outer, 8, 0)
     group = lax.broadcasted_iota(jnp.int32, (16, slots), 0) == place
-    lane = lax.broadcasted_iota(jnp.int32, (LANES, slots), 0) == (row & 15) * 8 + (col & 7)
+    lane = lax.broadcasted_iota(jnp.int32, (LANES, slots), 0) == ((row & 7) * 2 + ((row >> 3) & 1)) * 8 + (col & 7)
     parts = []
     for value in (rinv_ref[...], rinv_ref[...] * values_ref[...]):
         for _ in range(3):
@@ -52,12 +52,20 @@
     return pl.ds(col * 8, 8)
 
 
-def tiles_kernel(x_ref, u_ref, first_ref, last_ref):
+def tiles_kernel(x_ref, u_ref, first_ref, last_ref, block_ref, sems):
+    def arrival(s):
+        part = pl.ds(s * 8, 8)
+        return pltpu.make_async_copy(x_ref.at[part], block_ref.at[part], sems.at[s])
+
+    for s in range(16):
+        arrival(s).start()
+
     def strip(s, _):
         half = s // 8
         base = (s % 8) * 8
+        arrival(s).wait()
         for b in range(4):
-            block = x_ref[pl.ds(s * 8 + 2 * b, 2)].reshape(LANES, LANES)
+            block = block_ref[pl.ds(s * 8 + 2 * b, 2)].reshape(LANES, LANES)
             turned = (block * 0.5).T
             for j in range(8):
                 for g in range(2):
@@ -157,24 +165,18 @@
         sweep(load, store, list(range(15 - step, 15 + reach)), scale_of(step))
 
 
-def turned_rows(load, half, b, count):
-    return jnp.concatenate([load(j, half * 4 + b) for j in range(count)], axis=0).T
-
-
-def place_of(sub):
-    return pl.ds(sub, 8, stride=8)
-
-
-def gather_groups(part_ref, obs_ref, first_group, bh_ref, bl_ref, proj_ref):
+def gather_groups(part_ref, obs_ref, first_group, mean_ref, ah_ref, al_ref, bh_ref, bl_ref, proj_ref):
     def group(q, _):
         half = q // 4
         base = (q % 4) * 16
-        blocks = [
-            turned_rows(lambda j, sub: part_ref[base + j, place_of(sub), :], half, b, 16)
-            for b in range(4)
-        ]
+        blocks = []
+        for b in range(4):
+            place = pl.ds(half * 4 + b, 8, stride=8)
+            rows = [part_ref[base + 8 * p + j, place, :] for j in range(8) for p in range(2)]
+            blocks.append(jnp.concatenate(rows, axis=0).T)
         total = blocks[0] + blocks[1] + blocks[2] + blocks[3]
         mean = jnp.sum(total, axis=0, keepdims=True) * (1.0 / MEMBERS)
+        mean_ref[pl.ds(q, 1)] = mean
         weight = obs_ref[pl.ds(first_group + q, 1)]
         root = jnp.sqrt(weight)
         misfit = obs_ref[pl.ds(first_group + q + 16, 1)] - weight * mean
@@ -182,6 +184,7 @@
         for b in range(4):
             part = pl.ds(b * LANES, LANES)
             anomaly = blocks[b] - mean
+            ah_ref[part, lanes], al_ref[part, lanes] = split(anomaly)
             bh_ref[part, lanes], bl_ref[part, lanes] = split(anomaly * root)
             proj_ref[part] += anomaly * misfit
         return 0
@@ -191,49 +194,28 @@
     return dot(high, high, NT) + (dot(high, low, NT) + dot(low, high, NT))
 
 
-def inner_sums_kernel(inner_ref, obs_ref, matrix_ref, proj_ref, bh_ref, bl_ref):
+def inner_sums_kernel(inner_ref, obs_ref, matrix_ref, proj_ref, mean_ref, ah_ref, al_ref, bh_ref, bl_ref):
     proj_ref[...] = jnp.zeros_like(proj_ref)
-    matrix_ref[...] = gather_groups(inner_ref, obs_ref, 0, bh_ref, bl_ref, proj_ref)
+    matrix_ref[...] = gather_groups(
+        inner_ref, obs_ref, 0, mean_ref, ah_ref, al_ref, bh_ref, bl_ref, proj_ref
+    )
 
 
 def analysis_kernel(
-    u_ref, one_ref, two_ref, three_ref, inner_ref, west_ref, east_ref, obs_ref, matrix_ref, sums_ref,
+    u_ref, one_ref, two_ref, three_ref, west_ref, east_ref, obs_ref,
+    matrix_ref, sums_ref, mean_in_ref, ah_in_ref, al_in_ref,
     out_ref,
     w1_ref, w2_ref, w3_ref, e1_ref, e2_ref, e3_ref, outer_ref,
-    mean_ref, ah_ref, al_ref, bh_ref, bl_ref, proj_ref, t_ref, z_ref,
+    mean_ref, ah_ref, al_ref, bh_ref, bl_ref, proj_ref, y_ref, z_ref,
 ):
     outer_forecast(
         [u_ref, one_ref, two_ref, three_ref], west_ref, east_ref,
         [w1_ref, w2_ref, w3_ref], [e1_ref, e2_ref, e3_ref], outer_ref,
     )
     proj_ref[...] = sums_ref[...]
-    matrix = matrix_ref[...] + gather_groups(outer_ref, obs_ref, 8, bh_ref, bl_ref, proj_ref)
-    t_ref[...] = matrix
-
-    low_half = lax.broadcasted_iota(jnp.int32, (8, LANES), 0) < 4
-
-    def strip(s, _):
-        half = s // 8
-        base = (s % 8) * 8
-        blocks = []
-        for b in range(4):
-            rows = []
-            for j in range(8):
-                sub = place_of(half * 4 + b)
-                near = inner_ref[base + j, sub, :]
-                far = outer_ref[base + j, sub, :]
-                rows += [jnp.where(low_half, far, near), jnp.where(low_half, near, far)]
-            blocks.append(jnp.concatenate(rows, axis=0).T)
-        total = blocks[0] + blocks[1] + blocks[2] + blocks[3]
-        mean = jnp.sum(total, axis=0, keepdims=True) * (1.0 / MEMBERS)
-        mean_ref[pl.ds(s, 1)] = mean
-        lanes = pl.ds(pl.multiple_of(s * LANES, LANES), LANES)
-        for b in range(4):
-            part = pl.ds(b * LANES, LANES)
-            ah_ref[part, lanes], al_ref[part, lanes] = split(blocks[b] - mean)
-        return 0
-
-    lax.fori_loop(0, 16, strip, 0)
+    matrix = matrix_ref[...] + gather_groups(
+        outer_ref, obs_ref, 8, mean_ref, ah_ref, al_ref, bh_ref, bl_ref, proj_ref
+    )
 
     shape = (MEMBERS, MEMBERS)
     diagonal = lax.broadcasted_iota(jnp.int32, shape, 0) == lax.broadcasted_iota(jnp.int32, shape, 1)
@@ -241,34 +223,54 @@
     def plus(coefficient, x):
         return x + jnp.where(diagonal, coefficient, 0.0)
 
-    matrix = plus(1.0, t_ref[...])
+    matrix = plus(1.0, matrix)
     norm = jnp.sqrt(jnp.sum(jnp.sum(matrix * matrix, axis=0, keepdims=True), axis=1, keepdims=True))
-    t_ref[...] = matrix * (1.0 / norm)
-
+    y_ref[...] = matrix * (1.0 / norm)
+
+    identity = 1.0
     for pair in range(3):
-        t = t_ref[...]
+        y = y_ref[...]
+        t = y
+        if pair:
+            t = identity * y + dot3(split(z_ref[...]), split(y))
         ts = split(t)
         square = dot3(ts, ts)
-        inner = plus(1.6875, 0.0625 * square - 0.5625 * t)
-        both = plus(2.25, dot3(split(square), split(inner)) - 2.4375 * t)
-        us = split(both)
+        extra = 1.6875 * square - 2.4375 * t + dot3(split(square), split(0.0625 * square - 0.5625 * t))
+        es = split(extra)
         if pair < 2:
-            t_ref[...] = dot3(split(dot3(ts, us)), us)
-        z_ref[...] = both if pair == 0 else dot3(us, split(z_ref[...]))
-
-    root = z_ref[...] * (1.0 / jnp.sqrt(norm))
+            y_ref[...] = 2.25 * y + dot3(split(y), es)
+        if pair:
+            z = z_ref[...]
+            extra = 2.25 * z + identity * extra + dot3(es, split(z))
+        z_ref[...] = extra
+        identity = 2.25 * identity
+
+    root = plus(identity, z_ref[...]) * (1.0 / jnp.sqrt(norm))
     projected = jnp.sum(proj_ref[...], axis=1, keepdims=True)
     once = jnp.sum(root * projected, axis=0, keepdims=True)
     once = jnp.broadcast_to(once, (8, MEMBERS)).T[:, 0:1]
     shift = jnp.sum(root * once, axis=0, keepdims=True)
     weights = split(root + shift)
 
+    lane = lax.broadcasted_iota(jnp.int32, (MEMBERS, LANES), 1)
+    low = (lane & 7) < 4
+    even = (lane & 8) == 0
+
     def result_of(q, _):
-        lanes = pl.ds(pl.multiple_of(q * 256, 256), 256)
-        result = dot3(weights, (ah_ref[:, lanes], al_ref[:, lanes]))
-        for i in range(2):
-            piece = result[:, i * LANES : (i + 1) * LANES] + mean_ref[pl.ds(2 * q + i, 1)]
-            out_ref[pl.ds((2 * q + i) * 8, 8)] = piece.reshape(8, 64, LANES)
+        lanes = pl.ds(pl.multiple_of(q * LANES, LANES), LANES)
+        cells = [
+            jnp.concatenate([near[:, lanes], far[:, lanes]], axis=1)
+            for near, far in ((ah_in_ref, ah_ref), (al_in_ref, al_ref))
+        ]
+        result = dot3(weights, cells)
+        near = result[:, :LANES] + mean_in_ref[pl.ds(q, 1)]
+        far = result[:, LANES:] + mean_ref[pl.ds(q, 1)]
+        left = jnp.where(low, far, near)
+        right = jnp.where(low, near, far)
+        upper = jnp.where(even, left, pltpu.roll(right, 8, 1))
+        lower = jnp.where(even, pltpu.roll(left, LANES - 8, 1), right)
+        out_ref[pl.ds(q * 16, 8)] = upper.reshape(8, 64, LANES)
+        out_ref[pl.ds(q * 16 + 8, 8)] = lower.reshape(8, 64, LANES)
         return 0
 
     lax.fori_loop(0, 8, result_of, 0)
@@ -278,14 +280,17 @@
     return [pl.BlockSpec(memory_space=pltpu.VMEM) for _ in range(count)]
 
 
-def call(kernel, outs, scratch, limit, flops, name, *operands):
-    operands = [pltpu.with_memory_space_constraint(x, pltpu.VMEM) for x in operands]
+def in_vmem(x):
+    return pltpu.with_memory_space_constraint(x, pltpu.VMEM)
+
+
+def call(kernel, outs, scratch, limit, flops, name, *operands, specs=None):
     return pl.pallas_call(
         kernel,
-        out_shape=[pltpu.VMEM(shape, jnp.float32) for shape in outs],
-        in_specs=vmem(len(operands)),
+        out_shape=[pltpu.VMEM(*out) for out in outs],
+        in_specs=specs or vmem(len(operands)),
         out_specs=vmem(len(outs)),
-        scratch_shapes=[pltpu.VMEM(*shape) for shape in scratch],
+        scratch_shapes=scratch,
         compiler_params=pltpu.CompilerParams(vmem_limit_bytes=limit * 2**20),
         cost_estimate=pl.CostEstimate(flops=flops, transcendentals=0, bytes_accessed=2**20),
         name=name,
@@ -293,7 +298,7 @@
 
 
 def columns(count):
-    return (64, count * 8, LANES)
+    return (64, count * 8, LANES), jnp.float32
 
 
 def body(ensemble, obs_cells, obs_values, obs_rinv, obs_count):
@@ -315,30 +320,35 @@
         ensemble.reshape(regions, block, LANES), RING, split_axis=0, concat_axis=0, tiled=True
     )
     pieces_in, grids = lax.optimization_barrier((pieces_in, grids))
+    f32, bf16 = jnp.float32, jnp.bfloat16
     tiles, first, last = call(
-        tiles_kernel, [columns(16), columns(HALO), columns(HALO)], [], 8, unit, "tiles", pieces_in
+        tiles_kernel, [columns(16), columns(HALO), columns(HALO)],
+        [pltpu.VMEM((regions, block, LANES), f32), pltpu.SemaphoreType.DMA((16,))],
+        8, unit, "tiles", pieces_in, specs=[pl.BlockSpec(memory_space=pl.ANY)],
     )
     west = lax.ppermute(last, MESH, after)
     east = lax.ppermute(first, MESH, before)
-    levels = call(
-        inner_kernel, [columns(14), columns(12), columns(10), columns(8)], [], 2, 4 * unit, "inner", tiles
-    )
-
-    f32, bf16 = jnp.float32, jnp.bfloat16
-    half = ((MEMBERS, 1024), bf16)
-    whole = ((MEMBERS, 2048), bf16)
-    square = ((MEMBERS, MEMBERS), f32)
-    sums = (MEMBERS, LANES)
-    matrix, projected = call(
-        inner_sums_kernel, [square[0], sums], [half, half], 8, 6 * unit, "inner_sums", levels[3], grids
-    )
-    side = (columns(HALO), f32)
+    *levels, inner = call(
+        inner_kernel, [columns(14), columns(12), columns(10), columns(8)], [], 2, 4 * unit, "inner",
+        in_vmem(tiles),
+    )
+    half = (MEMBERS, 1024), bf16
+    square = (MEMBERS, MEMBERS), f32
+    sums = (MEMBERS, LANES), f32
+    means = (8, LANES), f32
+    partial = call(
+        inner_sums_kernel, [square, sums, means, half, half], [pltpu.VMEM(*half)] * 2,
+        8, 6 * unit, "inner_sums", in_vmem(inner), in_vmem(grids),
+    )
+    inputs = [tiles, *levels, west, east, grids, *partial]
     (analysed,) = call(
         analysis_kernel,
-        [(regions, block, LANES)],
-        [side] * 6
-        + [(columns(8), f32), ((16, LANES), f32), whole, whole, half, half, (sums, f32), square, square],
-        24, 30 * unit, "analysis", tiles, *levels, west, east, grids, matrix, projected,
+        [((regions, block, LANES), f32)],
+        [
+            pltpu.VMEM(*shape)
+            for shape in [columns(HALO)] * 6 + [columns(8), means] + [half] * 4 + [sums, square, square]
+        ],
+        24, 30 * unit, "analysis", *[in_vmem(x) for x in inputs],
     )
     returned = lax.all_to_all(analysed, RING, split_axis=0, concat_axis=0, tiled=True)
     return returned.reshape(ensemble.shape)

time: 180 us -> 177 us (0.983)
  Pallas kernels: 39.3 us -> 36.9 us
    pallas_call x4, Pallas kernels: 39 us -> 36.6 us  [call(): pl.pallas_call(kernel, out_shape=[pltpu.VMEM(*out) for out in outs], in_s...]
  transfers between devices with their start and end apart: 4 -> 4, of which waited for: 4 -> 4; matrix products, arithmetic and copies ran while one was open for 0% -> 0% of each run, Pallas kernels for 4% -> 5%
where the time goes in v2:
time: 177 us
  blocking collectives  66.3 us (37%)
  waiting for transfers between devices  52.5 us (30%)
  Pallas kernels  36.9 us (21%)
  starting transfers between devices  18.4 us (10%)
  local copies, waits for them, and re-layouts  2.02 us (1%)
    all_to_all x1, blocking collectives, body(): lax.all_to_all(analysed, RING, split_axis=0, concat_axis=0, tiled=True)  66.3 us
    pallas_call x4, Pallas kernels, call(): pl.pallas_call(kernel, out_shape=[pltpu.VMEM(*out) for out in outs], in_s...  36.6 us
    ppermute x1, waiting for transfers between devices, body(): grids = lax.ppermute(grids, MESH, list(enumerate(owner)))  33.6 us
    all_to_all x1, waiting for transfers between devices, body(): lax.all_to_all(ensemble.reshape(regions, block, LANES), RING, split_axis=...  13.1 us
    all_to_all x1, starting transfers between devices, body(): lax.all_to_all(ensemble.reshape(regions, block, LANES), RING, split_axis=...  12 us
    ppermute x1, starting transfers between devices, body(): grids = lax.ppermute(grids, MESH, list(enumerate(owner)))  5.06 us
  transfers between devices with their start and end apart: 4, of which 4 were waited for; matrix products, arithmetic and copies ran while one was open for 0% of the time, Pallas kernels for 5%

profile of v2, /device:TPU:1, one launch (start us, length us, event | category | flops | bytes accessed | tf_op | source)
XLA Modules:
  0.0 176.9 jit_solution(11909483972769937647)
XLA Ops:
  0.0 0.0 copy-start.2
  0.0 0.0 copy-start
  0.0 0.0 copy-start.1
  0.0 12.0 %all-to-all-start = ((f32[128,64,128]{2,1,0:T(8,128)}), f32[128,64,128]{2,1,0:T(8,128)}, u32[]{:S(2)}, u32[]{:S(2)}) async-start(f32[128,64,128]{2,1,0:T(8,128)} %bitcast.7), calls=%async_computation | async-start | bytes 8388608 | tf_op jit(solution)/shard_map/all_to_all | solution.py:319
  12.6 0.0 copy-done.2
  12.6 0.0 copy-done
  12.7 0.0 copy-done.1
  12.7 0.3 observations.1
  13.0 5.1 %collective-permute-start = (f32[32,128]{1,0:T(8,128)S(1)}, f32[32,128]{1,0:T(8,128)S(1)}, u32[]{:S(2)}, u32[]{:S(2)}) collective-permute-start(f32[32,128]{1,0:T(8,128)S(1)} %observations.1), channel_id=1, source_target_pairs={{0,0},{1,16},{2,32},{3,48},{4,64},{5,80},{6,96},{7,112},{8,1},{9,1... | collective-permute-start | bytes 49160 | tf_op jit(solution)/shard_map/ppermute | solution.py:318
  18.0 33.6 %collective-permute-done.obs_ref = f32[32,128]{1,0:T(8,128)S(1)} collective-permute-done((f32[32,128]{1,0:T(8,128)S(1)}, f32[32,128]{1,0:T(8,128)S(1)}, u32[]{:S(2)}, u32[]{:S(2)}) %collective-permute-start) | collective-permute-done | bytes 16416 | tf_op jit(solution)/shard_map/ppermute | solution.py:318
  51.6 13.1 %all-to-all-done.x_ref = f32[128,64,128]{2,1,0:T(8,128)} async-done(((f32[128,64,128]{2,1,0:T(8,128)}), f32[128,64,128]{2,1,0:T(8,128)}, u32[]{:S(2)}, u32[]{:S(2)}) %all-to-all-start) | async-done | bytes 4194336 | tf_op jit(solution)/shard_map/all_to_all | solution.py:319
  64.7 3.5 %tiles.1 = (f32[64,128,128]{2,1,0:T(8,128)S(1)}, f32[64,32,128]{2,1,0:T(8,128)S(1)}, f32[64,32,128]{2,1,0:T(8,128)S(1)}) custom-call(f32[128,64,128]{2,1,0:T(8,128)} %all-to-all-done.x_ref), custom_call_target="tpu_custom_call" | custom-call | flops 1000000000 | bytes 1048576 | tf_op jit(solution)/shard_map/tiles/pallas_call | solution.py:288
  68.1 1.0 collective-permute-start.1
  69.2 0.4 collective-permute-start.2
  69.5 3.7 %inner.1 = (f32[64,112,128]{2,1,0:T(8,128)S(1)}, f32[64,96,128]{2,1,0:T(8,128)S(1)}, f32[64,80,128]{2,1,0:T(8,128)S(1)}, f32[64,64,128]{2,1,0:T(8,128)S(1)}) custom-call(f32[64,128,128]{2,1,0:T(8,128)S(1)} %get-tuple-element.20.u_ref), custom_call_target="tpu_custom_call" | custom-call | flops 4000000000 | bytes 1048576 | tf_op jit(solution)/shard_map/inner/pallas_call | solution.py:288
  73.3 4.5 %inner_sums.1 = (f32[512,512]{1,0:T(8,128)S(1)}, f32[512,128]{1,0:T(8,128)S(1)}, f32[8,128]{1,0:T(8,128)S(1)}, bf16[512,1024]{1,0:T(8,128)(2,1)S(1)}, bf16[512,1024]{1,0:T(8,128)(2,1)S(1)}) custom-call(f32[64,64,128]{2,1,0:T(8,128)S(1)} %get-tuple-element.27.inner_ref, f32[32,128]{1,0:T(8,128)S(1)} %collective-permute-done.obs_ref), custom_call_target="tpu_custom_call" | custom-call | flops 6000000000 | bytes 1048576 | tf_op jit(solution)/shard_map/inner_sums/pallas_call | solution.py:288
  77.8 3.1 %collective-permute-done.1.west_ref = f32[64,32,128]{2,1,0:T(8,128)S(1)} collective-permute-done((f32[64,32,128]{2,1,0:T(8,128)S(1)}, f32[64,32,128]{2,1,0:T(8,128)S(1)}, u32[]{:S(2)}, u32[]{:S(2)}) %collective-permute-start.1) | collective-permute-done | bytes 1048608 | tf_op jit(solution)/shard_map/ppermute | solution.py:329
  80.9 2.8 %collective-permute-done.2.east_ref = f32[64,32,128]{2,1,0:T(8,128)S(1)} collective-permute-done((f32[64,32,128]{2,1,0:T(8,128)S(1)}, f32[64,32,128]{2,1,0:T(8,128)S(1)}, u32[]{:S(2)}, u32[]{:S(2)}) %collective-permute-start.2) | collective-permute-done | bytes 1048608 | tf_op jit(solution)/shard_map/ppermute | solution.py:330
  83.7 24.9 %analysis.1 = f32[128,64,128]{2,1,0:T(8,128)S(1)} custom-call(f32[64,128,128]{2,1,0:T(8,128)S(1)} %get-tuple-element.20.u_ref, f32[64,112,128]{2,1,0:T(8,128)S(1)} %get-tuple-element.21.one_ref, f32[64,96,128]{2,1,0:T(8,128)S(1)} %get-tuple-element.22.two_ref, f32[64,80,128]{2,1,0:T(8,128)S(1)} %get-tuple-element.23.three_ref, ...), custom_call_target="tpu_custom_call" | custom-call | flops 30000001024 | bytes 1048576 | tf_op jit(solution)/shard_map/analysis/pallas_call | solution.py:288
  108.6 66.3 %all_to_all.10 = f32[128,64,128]{2,1,0:T(8,128)S(1)} all-to-all(f32[128,64,128]{2,1,0:T(8,128)S(1)} %analysis.1), channel_id=1, replica_groups=mesh['mem'=8,'space'=16] {'space','mem'}, dimensions={0} | all-to-all | bytes 8388608 | tf_op jit(solution)/shard_map/all_to_all | solution.py:353
  174.9 2.0 %copy.9 = f32[128,64,1,128]{3,2,1,0:T(1,128)} copy(f32[128,64,1,128]{3,2,1,0:T(1,128)S(1)} %bitcast.6) | data formatting | bytes 8388608
  (1 shorter events, 0.0 us)
Async XLA Ops:
  0.0 12.6 %copy-start.2 = (f32[1,2048]{1,0:T(1,128)S(1)}, f32[1,2048]{1,0:T(1,128)}, u32[]{:S(2)}) copy-start(f32[1,2048]{1,0:T(1,128)} %param.8) | copy-start | bytes 24580
  0.0 12.6 %copy-start = (s32[1,2048]{1,0:T(1,128)S(1)}, s32[1,2048]{1,0:T(1,128)}, u32[]{:S(2)}) copy-start(s32[1,2048]{1,0:T(1,128)} %cells_ref.1) | copy-start | bytes 24580
  0.0 12.7 %copy-start.1 = (f32[1,2048]{1,0:T(1,128)S(1)}, f32[1,2048]{1,0:T(1,128)}, u32[]{:S(2)}) copy-start(f32[1,2048]{1,0:T(1,128)} %values_ref.1) | copy-start | bytes 24580
  0.0 64.7 %all-to-all-start = ((f32[128,64,128]{2,1,0:T(8,128)}), f32[128,64,128]{2,1,0:T(8,128)}, u32[]{:S(2)}, u32[]{:S(2)}) async-start(f32[128,64,128]{2,1,0:T(8,128)} %bitcast.7), calls=%async_computation | async-start | bytes 8388608 | tf_op jit(solution)/shard_map/all_to_all | solution.py:319
  13.0 38.6 %collective-permute-start = (f32[32,128]{1,0:T(8,128)S(1)}, f32[32,128]{1,0:T(8,128)S(1)}, u32[]{:S(2)}, u32[]{:S(2)}) collective-permute-start(f32[32,128]{1,0:T(8,128)S(1)} %observations.1), channel_id=1, source_target_pairs={{0,0},{1,16},{2,32},{3,48},{4,64},{5,80},{6,96},{7,112},{8,1},{9,1... | collective-permute-start | bytes 49160 | tf_op jit(solution)/shard_map/ppermute | solution.py:318
  68.1 12.8 %collective-permute-start.1 = (f32[64,32,128]{2,1,0:T(8,128)S(1)}, f32[64,32,128]{2,1,0:T(8,128)S(1)}, u32[]{:S(2)}, u32[]{:S(2)}) collective-permute-start(f32[64,32,128]{2,1,0:T(8,128)S(1)} %get-tuple-element.24), channel_id=1, source_target_pairs={{0,16},{16,32},{32,48},{48,64},{64,80},{80,96},{96,112},{112,1},{1... | collective-permute-start | bytes 3145736 | tf_op jit(solution)/shard_map/ppermute | solution.py:329
  69.2 14.5 %collective-permute-start.2 = (f32[64,32,128]{2,1,0:T(8,128)S(1)}, f32[64,32,128]{2,1,0:T(8,128)S(1)}, u32[]{:S(2)}, u32[]{:S(2)}) collective-permute-start(f32[64,32,128]{2,1,0:T(8,128)S(1)} %get-tuple-element.25), channel_id=1, source_target_pairs={{16,0},{32,16},{48,32},{64,48},{80,64},{96,80},{112,96},{1,112},{1... | collective-permute-start | bytes 3145736 | tf_op jit(solution)/shard_map/ppermute | solution.py:330

commit v3 on v2

--- a/solution.py
+++ b/solution.py
@@ -10,7 +10,21 @@
 HALO = STEPS
 LANES = 128
 MESH = ("mem", "space")
-RING = ("space", "mem")
+
+def column_strip(place):
+    return (place & 12) + ((place - (place >> 2)) & 3)
+
+
+def strip_column(strip):
+    return (strip & 12) + ((strip + (strip >> 2)) & 3)
+
+
+OWNER = [
+    (2 * ((k - place) & 3) + core) * 16 + column_strip(place)
+    for place in range(16)
+    for k in range(4)
+    for core in range(2)
+]
 
 
 NT = (((1,), (1,)), ((), ()))
@@ -60,12 +74,13 @@
     for s in range(16):
         arrival(s).start()
 
-    def strip(s, _):
+    def column(place, _):
+        s = column_strip(place)
         half = s // 8
         base = (s % 8) * 8
-        arrival(s).wait()
+        arrival(place).wait()
         for b in range(4):
-            block = block_ref[pl.ds(s * 8 + 2 * b, 2)].reshape(LANES, LANES)
+            block = block_ref[pl.ds(place * 8 + ((b + place) & 3) * 2, 2)].reshape(LANES, LANES)
             turned = (block * 0.5).T
             for j in range(8):
                 for g in range(2):
@@ -74,7 +89,7 @@
                     ]
         return 0
 
-    lax.fori_loop(0, 16, strip, 0)
+    lax.fori_loop(0, 16, column, 0)
 
     def edge(r, _):
         first_ref[r] = u_ref[r, 0 : HALO * 8, :]
@@ -269,8 +284,11 @@
         right = jnp.where(low, near, far)
         upper = jnp.where(even, left, pltpu.roll(right, 8, 1))
         lower = jnp.where(even, pltpu.roll(left, LANES - 8, 1), right)
-        out_ref[pl.ds(q * 16, 8)] = upper.reshape(8, 64, LANES)
-        out_ref[pl.ds(q * 16 + 8, 8)] = lower.reshape(8, 64, LANES)
+        for strip, values in ((2 * q, upper), (2 * q + 1, lower)):
+            place = strip_column(strip)
+            for b in range(4):
+                part = values[b * LANES : (b + 1) * LANES].reshape(2, 64, LANES)
+                out_ref[pl.ds(place * 8 + ((b + place) & 3) * 2, 2)] = part
         return 0
 
     lax.fori_loop(0, 8, result_of, 0)
@@ -303,9 +321,13 @@
 
 def body(ensemble, obs_cells, obs_values, obs_rinv, obs_count):
     regions, block = ensemble.shape[0], ensemble.shape[1]
-    owner = [(r % 8) * 16 + r // 8 for r in range(regions)]
-    after = [(owner[r], owner[(r + 1) % regions]) for r in range(regions)]
-    before = [(owner[(r + 1) % regions], owner[r]) for r in range(regions)]
+    following = OWNER[1:] + OWNER[:1]
+    after = list(zip(OWNER, following))
+    before = list(zip(following, OWNER))
+
+    def exchange(x):
+        return lax.all_to_all(x, MESH, split_axis=0, concat_axis=0, tiled=True, axis_index_groups=[OWNER])
+
     unit = 10**9
 
     slots = lax.broadcasted_iota(jnp.int32, obs_cells.shape, 1)
@@ -315,10 +337,8 @@
         obs_kernel, out_shape=pltpu.VMEM((32, LANES), jnp.float32), in_specs=vmem(3), out_specs=vmem(1)[0],
         compiler_params=pltpu.CompilerParams(vmem_limit_bytes=4 * 2**20), name="observations",
     )(obs_cells, rinv, obs_values)
-    grids = lax.ppermute(grids, MESH, list(enumerate(owner)))
-    pieces_in = lax.all_to_all(
-        ensemble.reshape(regions, block, LANES), RING, split_axis=0, concat_axis=0, tiled=True
-    )
+    grids = lax.ppermute(grids, MESH, list(enumerate(OWNER)))
+    pieces_in = exchange(ensemble.reshape(regions, block, LANES))
     pieces_in, grids = lax.optimization_barrier((pieces_in, grids))
     f32, bf16 = jnp.float32, jnp.bfloat16
     tiles, first, last = call(
@@ -350,8 +370,7 @@
         ],
         24, 30 * unit, "analysis", *[in_vmem(x) for x in inputs],
     )
-    returned = lax.all_to_all(analysed, RING, split_axis=0, concat_axis=0, tiled=True)
-    return returned.reshape(ensemble.shape)
+    return exchange(analysed).reshape(ensemble.shape)
 
 
 def solution(mesh):

time: 177 us -> 172 us (0.972)
  blocking collectives: 66.3 us -> 60.7 us
  waiting for transfers between devices: 52.5 us -> 48.3 us
  starting transfers between devices: 18.4 us -> 22 us
    all_to_all x1, waiting for transfers between devices: 13.1 us -> 5.2 us  [exchange(): lax.all_to_all(x, MESH, split_axis=0, concat_axis=0, tiled=True, axis_ind...]
    all_to_all x1, blocking collectives: 66.3 us -> 60.7 us  [exchange(): lax.all_to_all(x, MESH, split_axis=0, concat_axis=0, tiled=True, axis_ind...]
    ppermute x1, waiting for transfers between devices: 33.6 us -> 36.9 us  [body(): grids = lax.ppermute(grids, MESH, list(enumerate(OWNER)))]
    ppermute x1, starting transfers between devices: 5.06 us -> 7.98 us  [body(): grids = lax.ppermute(grids, MESH, list(enumerate(OWNER)))]
where the time goes in v3:
time: 172 us; the launch traced here: 171 us
  blocking collectives  60.7 us (35%)
  waiting for transfers between devices  48.3 us (28%)
  Pallas kernels  37.1 us (22%)
  starting transfers between devices  22 us (13%)
  local copies, waits for them, and re-layouts  2.02 us (1%)
    all_to_all x1, blocking collectives, exchange(): lax.all_to_all(x, MESH, split_axis=0, concat_axis=0, tiled=True, axis_ind...  60.7 us
    ppermute x1, waiting for transfers between devices, body(): grids = lax.ppermute(grids, MESH, list(enumerate(OWNER)))  36.9 us
    pallas_call x4, Pallas kernels, call(): pl.pallas_call(kernel, out_shape=[pltpu.VMEM(*out) for out in outs], in_s...  36.8 us
    all_to_all x1, starting transfers between devices, exchange(): lax.all_to_all(x, MESH, split_axis=0, concat_axis=0, tiled=True, axis_ind...  12 us
    ppermute x1, starting transfers between devices, body(): grids = lax.ppermute(grids, MESH, list(enumerate(OWNER)))  7.98 us
    all_to_all x1, waiting for transfers between devices, exchange(): lax.all_to_all(x, MESH, split_axis=0, concat_axis=0, tiled=True, axis_ind...  5.2 us
    ppermute x1, waiting for transfers between devices, body(): west = lax.ppermute(last, MESH, after)  3.47 us
  transfers between devices with their start and end apart: 4, of which 4 were waited for; matrix products, arithmetic and copies ran while one was open for 0% of the time, Pallas kernels for 5%

profile of v3, /device:TPU:1, one launch (start us, length us, event | category | flops | bytes accessed | tf_op | source)
XLA Modules:
  0.0 170.8 jit_solution(1904149643233453613)
XLA Ops:
  0.0 0.0 copy-start.2
  0.0 0.0 copy-start
  0.0 0.0 copy-start.1
  0.0 12.0 %all-to-all-start = ((f32[128,64,128]{2,1,0:T(8,128)}), f32[128,64,128]{2,1,0:T(8,128)}, u32[]{:S(2)}, u32[]{:S(2)}) async-start(f32[128,64,128]{2,1,0:T(8,128)} %bitcast.7), calls=%async_computation | async-start | bytes 8388608 | tf_op jit(solution)/shard_map/all_to_all | solution.py:329
  12.6 0.0 copy-done.2
  12.6 0.0 copy-done
  12.7 0.0 copy-done.1
  12.7 0.3 observations.1
  13.0 8.0 %collective-permute-start = (f32[32,128]{1,0:T(8,128)S(1)}, f32[32,128]{1,0:T(8,128)S(1)}, u32[]{:S(2)}, u32[]{:S(2)}) collective-permute-start(f32[32,128]{1,0:T(8,128)S(1)} %observations.1), channel_id=1, source_target_pairs={{0,0},{1,16},{2,32},{3,48},{4,64},{5,80},{6,96},{7,112},{8,97},{9,... | collective-permute-start | bytes 49160 | tf_op jit(solution)/shard_map/ppermute | solution.py:340
  21.0 36.9 %collective-permute-done.obs_ref = f32[32,128]{1,0:T(8,128)S(1)} collective-permute-done((f32[32,128]{1,0:T(8,128)S(1)}, f32[32,128]{1,0:T(8,128)S(1)}, u32[]{:S(2)}, u32[]{:S(2)}) %collective-permute-start) | collective-permute-done | bytes 16416 | tf_op jit(solution)/shard_map/ppermute | solution.py:340
  57.9 5.2 %all-to-all-done.x_ref = f32[128,64,128]{2,1,0:T(8,128)} async-done(((f32[128,64,128]{2,1,0:T(8,128)}), f32[128,64,128]{2,1,0:T(8,128)}, u32[]{:S(2)}, u32[]{:S(2)}) %all-to-all-start) | async-done | bytes 4194336 | tf_op jit(solution)/shard_map/all_to_all | solution.py:329
  63.1 3.5 %tiles.1 = (f32[64,128,128]{2,1,0:T(8,128)S(1)}, f32[64,32,128]{2,1,0:T(8,128)S(1)}, f32[64,32,128]{2,1,0:T(8,128)S(1)}) custom-call(f32[128,64,128]{2,1,0:T(8,128)} %all-to-all-done.x_ref), custom_call_target="tpu_custom_call" | custom-call | flops 1000000000 | bytes 1048576 | tf_op jit(solution)/shard_map/tiles/pallas_call | solution.py:306
  66.5 2.1 %collective-permute-start.1 = (f32[64,32,128]{2,1,0:T(8,128)S(1)}, f32[64,32,128]{2,1,0:T(8,128)S(1)}, u32[]{:S(2)}, u32[]{:S(2)}) collective-permute-start(f32[64,32,128]{2,1,0:T(8,128)S(1)} %get-tuple-element.24), channel_id=1, source_target_pairs={{0,16},{16,32},{32,48},{48,64},{64,80},{80,96},{96,112},{112,97},{... | collective-permute-start | bytes 3145736 | tf_op jit(solution)/shard_map/ppermute | solution.py:349
  68.6 0.0 collective-permute-start.2
  68.6 3.7 %inner.1 = (f32[64,112,128]{2,1,0:T(8,128)S(1)}, f32[64,96,128]{2,1,0:T(8,128)S(1)}, f32[64,80,128]{2,1,0:T(8,128)S(1)}, f32[64,64,128]{2,1,0:T(8,128)S(1)}) custom-call(f32[64,128,128]{2,1,0:T(8,128)S(1)} %get-tuple-element.20.u_ref), custom_call_target="tpu_custom_call" | custom-call | flops 4000000000 | bytes 1048576 | tf_op jit(solution)/shard_map/inner/pallas_call | solution.py:306
  72.4 4.5 %inner_sums.1 = (f32[512,512]{1,0:T(8,128)S(1)}, f32[512,128]{1,0:T(8,128)S(1)}, f32[8,128]{1,0:T(8,128)S(1)}, bf16[512,1024]{1,0:T(8,128)(2,1)S(1)}, bf16[512,1024]{1,0:T(8,128)(2,1)S(1)}) custom-call(f32[64,64,128]{2,1,0:T(8,128)S(1)} %get-tuple-element.27.inner_ref, f32[32,128]{1,0:T(8,128)S(1)} %collective-permute-done.obs_ref), custom_call_target="tpu_custom_call" | custom-call | flops 6000000000 | bytes 1048576 | tf_op jit(solution)/shard_map/inner_sums/pallas_call | solution.py:306
  76.9 3.5 %collective-permute-done.1.west_ref = f32[64,32,128]{2,1,0:T(8,128)S(1)} collective-permute-done((f32[64,32,128]{2,1,0:T(8,128)S(1)}, f32[64,32,128]{2,1,0:T(8,128)S(1)}, u32[]{:S(2)}, u32[]{:S(2)}) %collective-permute-start.1) | collective-permute-done | bytes 1048608 | tf_op jit(solution)/shard_map/ppermute | solution.py:349
  80.4 2.7 %collective-permute-done.2.east_ref = f32[64,32,128]{2,1,0:T(8,128)S(1)} collective-permute-done((f32[64,32,128]{2,1,0:T(8,128)S(1)}, f32[64,32,128]{2,1,0:T(8,128)S(1)}, u32[]{:S(2)}, u32[]{:S(2)}) %collective-permute-start.2) | collective-permute-done | bytes 1048608 | tf_op jit(solution)/shard_map/ppermute | solution.py:350
  83.1 25.0 %analysis.1 = f32[128,64,128]{2,1,0:T(8,128)S(1)} custom-call(f32[64,128,128]{2,1,0:T(8,128)S(1)} %get-tuple-element.20.u_ref, f32[64,112,128]{2,1,0:T(8,128)S(1)} %get-tuple-element.21.one_ref, f32[64,96,128]{2,1,0:T(8,128)S(1)} %get-tuple-element.22.two_ref, f32[64,80,128]{2,1,0:T(8,128)S(1)} %get-tuple-element.23.three_ref, ...), custom_call_target="tpu_custom_call" | custom-call | flops 30000001024 | bytes 1048576 | tf_op jit(solution)/shard_map/analysis/pallas_call | solution.py:306
  108.1 60.7 %all_to_all.10 = f32[128,64,128]{2,1,0:T(8,128)S(1)} all-to-all(f32[128,64,128]{2,1,0:T(8,128)S(1)} %analysis.1), channel_id=1, replica_groups={{0,16,32,48,64,80,96,112,97,113,1,17,33,49,65,81,66,82,98,114,2,18,34,5..., dimensions={0} | all-to-all | bytes 8388608 | tf_op jit(solution)/shard_map/all_to_all | solution.py:329
  168.8 2.0 %copy.9 = f32[128,64,1,128]{3,2,1,0:T(1,128)} copy(f32[128,64,1,128]{3,2,1,0:T(1,128)S(1)} %bitcast.6) | data formatting | bytes 8388608
  (1 shorter events, 0.0 us)
Async XLA Ops:
  0.0 12.6 %copy-start.2 = (f32[1,2048]{1,0:T(1,128)S(1)}, f32[1,2048]{1,0:T(1,128)}, u32[]{:S(2)}) copy-start(f32[1,2048]{1,0:T(1,128)} %param.8) | copy-start | bytes 24580
  0.0 12.6 %copy-start = (s32[1,2048]{1,0:T(1,128)S(1)}, s32[1,2048]{1,0:T(1,128)}, u32[]{:S(2)}) copy-start(s32[1,2048]{1,0:T(1,128)} %cells_ref.1) | copy-start | bytes 24580
  0.0 12.7 %copy-start.1 = (f32[1,2048]{1,0:T(1,128)S(1)}, f32[1,2048]{1,0:T(1,128)}, u32[]{:S(2)}) copy-start(f32[1,2048]{1,0:T(1,128)} %values_ref.1) | copy-start | bytes 24580
  0.0 63.0 %all-to-all-start = ((f32[128,64,128]{2,1,0:T(8,128)}), f32[128,64,128]{2,1,0:T(8,128)}, u32[]{:S(2)}, u32[]{:S(2)}) async-start(f32[128,64,128]{2,1,0:T(8,128)} %bitcast.7), calls=%async_computation | async-start | bytes 8388608 | tf_op jit(solution)/shard_map/all_to_all | solution.py:329
  13.0 44.9 %collective-permute-start = (f32[32,128]{1,0:T(8,128)S(1)}, f32[32,128]{1,0:T(8,128)S(1)}, u32[]{:S(2)}, u32[]{:S(2)}) collective-permute-start(f32[32,128]{1,0:T(8,128)S(1)} %observations.1), channel_id=1, source_target_pairs={{0,0},{1,16},{2,32},{3,48},{4,64},{5,80},{6,96},{7,112},{8,97},{9,... | collective-permute-start | bytes 49160 | tf_op jit(solution)/shard_map/ppermute | solution.py:340
  66.5 13.8 %collective-permute-start.1 = (f32[64,32,128]{2,1,0:T(8,128)S(1)}, f32[64,32,128]{2,1,0:T(8,128)S(1)}, u32[]{:S(2)}, u32[]{:S(2)}) collective-permute-start(f32[64,32,128]{2,1,0:T(8,128)S(1)} %get-tuple-element.24), channel_id=1, source_target_pairs={{0,16},{16,32},{32,48},{48,64},{64,80},{80,96},{96,112},{112,97},{... | collective-permute-start | bytes 3145736 | tf_op jit(solution)/shard_map/ppermute | solution.py:349
  68.6 14.5 %collective-permute-start.2 = (f32[64,32,128]{2,1,0:T(8,128)S(1)}, f32[64,32,128]{2,1,0:T(8,128)S(1)}, u32[]{:S(2)}, u32[]{:S(2)}) collective-permute-start(f32[64,32,128]{2,1,0:T(8,128)S(1)} %get-tuple-element.25), channel_id=1, source_target_pairs={{16,0},{32,16},{48,32},{64,48},{80,64},{96,80},{112,96},{97,112},{... | collective-permute-start | bytes 3145736 | tf_op jit(solution)/shard_map/ppermute | solution.py:350

commit v4 on v3

--- a/solution.py
+++ b/solution.py
@@ -99,17 +99,20 @@
     lax.fori_loop(0, 64, edge, 0, unroll=4)
 
 
-def sweep(load, store, columns, scale):
-    width = len(columns)
+def sweep(load, store, groups, scale):
+    columns = [k for group in groups for k in group]
 
     def row(r, n, c, s):
-        west = load(r, columns[0] - 1)
-        east = load(r, columns[-1] + 1)
-        around = [west] + list(c) + [east]
-        for i in range(width):
-            p = around[i + 2] + s[i]
-            q = around[i] + n[i]
-            store(r, columns[i], scale * ((c[i] + (p + q)) - c[i] * (p - q)))
+        first = 0
+        for group in groups:
+            last = first + len(group)
+            around = [load(r, group[0] - 1), *c[first:last], load(r, group[-1] + 1)]
+            for i, k in enumerate(group):
+                at_k = c[first + i]
+                p = around[i + 2] + s[first + i]
+                q = around[i] + n[first + i]
+                store(r, k, scale * ((at_k + (p + q)) - at_k * (p - q)))
+            first = last
 
     def body(r, carry):
         n, c = carry
@@ -149,7 +152,7 @@
                 inner_ref[r, at(col & 7), :] = value
 
         for columns in pieces(low, high, 8):
-            sweep(load, store, columns, scale_of(step))
+            sweep(load, store, [columns], scale_of(step))
 
 
 def outer_forecast(levels, west_ref, east_ref, wests, easts, outer_ref):
@@ -176,8 +179,8 @@
             else:
                 easts[step][r, at(col - 15 + step), :] = value
 
-        sweep(load, store, list(range(1 - reach, step + 1)), scale_of(step))
-        sweep(load, store, list(range(15 - step, 15 + reach)), scale_of(step))
+        sides = [list(range(1 - reach, step + 1)), list(range(15 - step, 15 + reach))]
+        sweep(load, store, sides, scale_of(step))
 
 
 def gather_groups(part_ref, obs_ref, first_group, mean_ref, ah_ref, al_ref, bh_ref, bl_ref, proj_ref):
@@ -206,7 +209,8 @@
 
     lax.fori_loop(0, 8, group, 0)
     high, low = bh_ref[...], bl_ref[...]
-    return dot(high, high, NT) + (dot(high, low, NT) + dot(low, high, NT))
+    cross = dot(high, low, NT)
+    return dot(high, high, NT) + (cross + cross.T)
 
 
 def inner_sums_kernel(inner_ref, obs_ref, matrix_ref, proj_ref, mean_ref, ah_ref, al_ref, bh_ref, bl_ref):
@@ -291,7 +295,7 @@
                 out_ref[pl.ds(place * 8 + ((b + place) & 3) * 2, 2)] = part
         return 0
 
-    lax.fori_loop(0, 8, result_of, 0)
+    lax.fori_loop(0, 8, result_of, 0, unroll=2)
 
 
 def vmem(count):

time: 172 us -> 171 us (level)
  Pallas kernels: 37.1 us -> 35.3 us
    pallas_call x4, Pallas kernels: 36.8 us -> 35 us  [call(): pl.pallas_call(kernel, out_shape=[pltpu.VMEM(*out) for out in outs], in_s...]
where the time goes in v4:
time: 171 us; the launch traced here: 170 us
  blocking collectives  60.7 us (35%)
  waiting for transfers between devices  48.8 us (29%)
  Pallas kernels  35.3 us (21%)
  starting transfers between devices  22 us (13%)
  local copies, waits for them, and re-layouts  2.02 us (1%)
    all_to_all x1, blocking collectives, exchange(): lax.all_to_all(x, MESH, split_axis=0, concat_axis=0, tiled=True, axis_ind...  60.7 us
    ppermute x1, waiting for transfers between devices, body(): grids = lax.ppermute(grids, MESH, list(enumerate(OWNER)))  36.9 us
    pallas_call x4, Pallas kernels, call(): pl.pallas_call(kernel, out_shape=[pltpu.VMEM(*out) for out in outs], in_s...  35 us
    all_to_all x1, starting transfers between devices, exchange(): lax.all_to_all(x, MESH, split_axis=0, concat_axis=0, tiled=True, axis_ind...  12 us
    ppermute x1, starting transfers between devices, body(): grids = lax.ppermute(grids, MESH, list(enumerate(OWNER)))  7.98 us
    all_to_all x1, waiting for transfers between devices, exchange(): lax.all_to_all(x, MESH, split_axis=0, concat_axis=0, tiled=True, axis_ind...  5.2 us
    ppermute x1, waiting for transfers between devices, body(): west = lax.ppermute(last, MESH, after)  4.01 us
  transfers between devices with their start and end apart: 4, of which 4 were waited for; matrix products, arithmetic and copies ran while one was open for 0% of the time, Pallas kernels for 5%

profile of v4, /device:TPU:1, one launch (start us, length us, event | category | flops | bytes accessed | tf_op | source)
XLA Modules:
  0.0 169.6 jit_solution(15267563218333747743)
XLA Ops:
  0.0 0.0 copy-start.2
  0.0 0.0 copy-start
  0.0 0.0 copy-start.1
  0.0 12.0 %all-to-all-start = ((f32[128,64,128]{2,1,0:T(8,128)}), f32[128,64,128]{2,1,0:T(8,128)}, u32[]{:S(2)}, u32[]{:S(2)}) async-start(f32[128,64,128]{2,1,0:T(8,128)} %bitcast.7), calls=%async_computation | async-start | bytes 8388608 | tf_op jit(solution)/shard_map/all_to_all | solution.py:333
  12.6 0.0 copy-done.2
  12.6 0.0 copy-done
  12.7 0.0 copy-done.1
  12.7 0.3 observations.1
  13.0 8.0 %collective-permute-start = (f32[32,128]{1,0:T(8,128)S(1)}, f32[32,128]{1,0:T(8,128)S(1)}, u32[]{:S(2)}, u32[]{:S(2)}) collective-permute-start(f32[32,128]{1,0:T(8,128)S(1)} %observations.1), channel_id=1, source_target_pairs={{0,0},{1,16},{2,32},{3,48},{4,64},{5,80},{6,96},{7,112},{8,97},{9,... | collective-permute-start | bytes 49160 | tf_op jit(solution)/shard_map/ppermute | solution.py:344
  21.0 36.9 %collective-permute-done.obs_ref = f32[32,128]{1,0:T(8,128)S(1)} collective-permute-done((f32[32,128]{1,0:T(8,128)S(1)}, f32[32,128]{1,0:T(8,128)S(1)}, u32[]{:S(2)}, u32[]{:S(2)}) %collective-permute-start) | collective-permute-done | bytes 16416 | tf_op jit(solution)/shard_map/ppermute | solution.py:344
  57.9 5.2 %all-to-all-done.x_ref = f32[128,64,128]{2,1,0:T(8,128)} async-done(((f32[128,64,128]{2,1,0:T(8,128)}), f32[128,64,128]{2,1,0:T(8,128)}, u32[]{:S(2)}, u32[]{:S(2)}) %all-to-all-start) | async-done | bytes 4194336 | tf_op jit(solution)/shard_map/all_to_all | solution.py:333
  63.1 3.5 %tiles.1 = (f32[64,128,128]{2,1,0:T(8,128)S(1)}, f32[64,32,128]{2,1,0:T(8,128)S(1)}, f32[64,32,128]{2,1,0:T(8,128)S(1)}) custom-call(f32[128,64,128]{2,1,0:T(8,128)} %all-to-all-done.x_ref), custom_call_target="tpu_custom_call" | custom-call | flops 1000000000 | bytes 1048576 | tf_op jit(solution)/shard_map/tiles/pallas_call | solution.py:310
  66.5 2.1 %collective-permute-start.1 = (f32[64,32,128]{2,1,0:T(8,128)S(1)}, f32[64,32,128]{2,1,0:T(8,128)S(1)}, u32[]{:S(2)}, u32[]{:S(2)}) collective-permute-start(f32[64,32,128]{2,1,0:T(8,128)S(1)} %get-tuple-element.24), channel_id=1, source_target_pairs={{0,16},{16,32},{32,48},{48,64},{64,80},{80,96},{96,112},{112,97},{... | collective-permute-start | bytes 3145736 | tf_op jit(solution)/shard_map/ppermute | solution.py:353
  68.6 0.0 collective-permute-start.2
  68.6 3.7 %inner.1 = (f32[64,112,128]{2,1,0:T(8,128)S(1)}, f32[64,96,128]{2,1,0:T(8,128)S(1)}, f32[64,80,128]{2,1,0:T(8,128)S(1)}, f32[64,64,128]{2,1,0:T(8,128)S(1)}) custom-call(f32[64,128,128]{2,1,0:T(8,128)S(1)} %get-tuple-element.20.u_ref), custom_call_target="tpu_custom_call" | custom-call | flops 4000000000 | bytes 1048576 | tf_op jit(solution)/shard_map/inner/pallas_call | solution.py:310
  72.4 4.0 %inner_sums.1 = (f32[512,512]{1,0:T(8,128)S(1)}, f32[512,128]{1,0:T(8,128)S(1)}, f32[8,128]{1,0:T(8,128)S(1)}, bf16[512,1024]{1,0:T(8,128)(2,1)S(1)}, bf16[512,1024]{1,0:T(8,128)(2,1)S(1)}) custom-call(f32[64,64,128]{2,1,0:T(8,128)S(1)} %get-tuple-element.27.inner_ref, f32[32,128]{1,0:T(8,128)S(1)} %collective-permute-done.obs_ref), custom_call_target="tpu_custom_call" | custom-call | flops 6000000000 | bytes 1048576 | tf_op jit(solution)/shard_map/inner_sums/pallas_call | solution.py:310
  76.4 4.0 %collective-permute-done.1.west_ref = f32[64,32,128]{2,1,0:T(8,128)S(1)} collective-permute-done((f32[64,32,128]{2,1,0:T(8,128)S(1)}, f32[64,32,128]{2,1,0:T(8,128)S(1)}, u32[]{:S(2)}, u32[]{:S(2)}) %collective-permute-start.1) | collective-permute-done | bytes 1048608 | tf_op jit(solution)/shard_map/ppermute | solution.py:353
  80.4 2.7 %collective-permute-done.2.east_ref = f32[64,32,128]{2,1,0:T(8,128)S(1)} collective-permute-done((f32[64,32,128]{2,1,0:T(8,128)S(1)}, f32[64,32,128]{2,1,0:T(8,128)S(1)}, u32[]{:S(2)}, u32[]{:S(2)}) %collective-permute-start.2) | collective-permute-done | bytes 1048608 | tf_op jit(solution)/shard_map/ppermute | solution.py:354
  83.1 23.8 %analysis.1 = f32[128,64,128]{2,1,0:T(8,128)S(1)} custom-call(f32[64,128,128]{2,1,0:T(8,128)S(1)} %get-tuple-element.20.u_ref, f32[64,112,128]{2,1,0:T(8,128)S(1)} %get-tuple-element.21.one_ref, f32[64,96,128]{2,1,0:T(8,128)S(1)} %get-tuple-element.22.two_ref, f32[64,80,128]{2,1,0:T(8,128)S(1)} %get-tuple-element.23.three_ref, ...), custom_call_target="tpu_custom_call" | custom-call | flops 30000001024 | bytes 1048576 | tf_op jit(solution)/shard_map/analysis/pallas_call | solution.py:310
  106.9 60.7 %all_to_all.10 = f32[128,64,128]{2,1,0:T(8,128)S(1)} all-to-all(f32[128,64,128]{2,1,0:T(8,128)S(1)} %analysis.1), channel_id=1, replica_groups={{0,16,32,48,64,80,96,112,97,113,1,17,33,49,65,81,66,82,98,114,2,18,34,5..., dimensions={0} | all-to-all | bytes 8388608 | tf_op jit(solution)/shard_map/all_to_all | solution.py:333
  167.6 2.0 %copy.9 = f32[128,64,1,128]{3,2,1,0:T(1,128)} copy(f32[128,64,1,128]{3,2,1,0:T(1,128)S(1)} %bitcast.6) | data formatting | bytes 8388608
  (1 shorter events, 0.0 us)
Async XLA Ops:
  0.0 12.6 %copy-start.2 = (f32[1,2048]{1,0:T(1,128)S(1)}, f32[1,2048]{1,0:T(1,128)}, u32[]{:S(2)}) copy-start(f32[1,2048]{1,0:T(1,128)} %param.8) | copy-start | bytes 24580
  0.0 12.6 %copy-start = (s32[1,2048]{1,0:T(1,128)S(1)}, s32[1,2048]{1,0:T(1,128)}, u32[]{:S(2)}) copy-start(s32[1,2048]{1,0:T(1,128)} %cells_ref.1) | copy-start | bytes 24580
  0.0 12.7 %copy-start.1 = (f32[1,2048]{1,0:T(1,128)S(1)}, f32[1,2048]{1,0:T(1,128)}, u32[]{:S(2)}) copy-start(f32[1,2048]{1,0:T(1,128)} %values_ref.1) | copy-start | bytes 24580
  0.0 63.0 %all-to-all-start = ((f32[128,64,128]{2,1,0:T(8,128)}), f32[128,64,128]{2,1,0:T(8,128)}, u32[]{:S(2)}, u32[]{:S(2)}) async-start(f32[128,64,128]{2,1,0:T(8,128)} %bitcast.7), calls=%async_computation | async-start | bytes 8388608 | tf_op jit(solution)/shard_map/all_to_all | solution.py:333
  13.0 44.9 %collective-permute-start = (f32[32,128]{1,0:T(8,128)S(1)}, f32[32,128]{1,0:T(8,128)S(1)}, u32[]{:S(2)}, u32[]{:S(2)}) collective-permute-start(f32[32,128]{1,0:T(8,128)S(1)} %observations.1), channel_id=1, source_target_pairs={{0,0},{1,16},{2,32},{3,48},{4,64},{5,80},{6,96},{7,112},{8,97},{9,... | collective-permute-start | bytes 49160 | tf_op jit(solution)/shard_map/ppermute | solution.py:344
  66.5 13.8 %collective-permute-start.1 = (f32[64,32,128]{2,1,0:T(8,128)S(1)}, f32[64,32,128]{2,1,0:T(8,128)S(1)}, u32[]{:S(2)}, u32[]{:S(2)}) collective-permute-start(f32[64,32,128]{2,1,0:T(8,128)S(1)} %get-tuple-element.24), channel_id=1, source_target_pairs={{0,16},{16,32},{32,48},{48,64},{64,80},{80,96},{96,112},{112,97},{... | collective-permute-start | bytes 3145736 | tf_op jit(solution)/shard_map/ppermute | solution.py:353
  68.6 14.5 %collective-permute-start.2 = (f32[64,32,128]{2,1,0:T(8,128)S(1)}, f32[64,32,128]{2,1,0:T(8,128)S(1)}, u32[]{:S(2)}, u32[]{:S(2)}) collective-permute-start(f32[64,32,128]{2,1,0:T(8,128)S(1)} %get-tuple-element.25), channel_id=1, source_target_pairs={{16,0},{32,16},{48,32},{64,48},{80,64},{96,80},{112,96},{97,112},{... | collective-permute-start | bytes 3145736 | tf_op jit(solution)/shard_map/ppermute | solution.py:354

commit v5 on v4

--- a/solution.py
+++ b/solution.py
@@ -41,6 +41,14 @@
 
 def dot3(a, b):
     return dot(a[0], b[0]) + (dot(a[0], b[1]) + dot(a[1], b[0]))
+
+
+def symmetric3(a, b):
+    middle = MEMBERS // 2
+    top = dot3([x[:middle] for x in a], b)
+    corner = dot3([x[middle:] for x in a], [x[:, middle:] for x in b])
+    bottom = jnp.concatenate([top[:, middle:].T, corner], axis=1)
+    return jnp.concatenate([top, bottom], axis=0)
 
 
 def obs_kernel(cells_ref, rinv_ref, values_ref, out_ref):
@@ -251,16 +259,16 @@
         y = y_ref[...]
         t = y
         if pair:
-            t = identity * y + dot3(split(z_ref[...]), split(y))
+            t = identity * y + symmetric3(split(z_ref[...]), split(y))
         ts = split(t)
-        square = dot3(ts, ts)
-        extra = 1.6875 * square - 2.4375 * t + dot3(split(square), split(0.0625 * square - 0.5625 * t))
+        square = symmetric3(ts, ts)
+        extra = 1.6875 * square - 2.4375 * t + symmetric3(split(square), split(0.0625 * square - 0.5625 * t))
         es = split(extra)
         if pair < 2:
-            y_ref[...] = 2.25 * y + dot3(split(y), es)
+            y_ref[...] = 2.25 * y + symmetric3(split(y), es)
         if pair:
             z = z_ref[...]
-            extra = 2.25 * z + identity * extra + dot3(es, split(z))
+            extra = 2.25 * z + identity * extra + symmetric3(es, split(z))
         z_ref[...] = extra
         identity = 2.25 * identity
 

time: 171 us -> 170 us (level)
  no operation moved by 1% of the time
where the time goes in v5:
time: 170 us; the launch traced here: 168 us
  blocking collectives  60.7 us (36%)
  waiting for transfers between devices  48.8 us (29%)
  Pallas kernels  34 us (20%)
  starting transfers between devices  22 us (13%)
  local copies, waits for them, and re-layouts  2.02 us (1%)
    all_to_all x1, blocking collectives, exchange(): lax.all_to_all(x, MESH, split_axis=0, concat_axis=0, tiled=True, axis_ind...  60.7 us
    ppermute x1, waiting for transfers between devices, body(): grids = lax.ppermute(grids, MESH, list(enumerate(OWNER)))  36.9 us
    pallas_call x4, Pallas kernels, call(): pl.pallas_call(kernel, out_shape=[pltpu.VMEM(*out) for out in outs], in_s...  33.8 us
    all_to_all x1, starting transfers between devices, exchange(): lax.all_to_all(x, MESH, split_axis=0, concat_axis=0, tiled=True, axis_ind...  12 us
    ppermute x1, starting transfers between devices, body(): grids = lax.ppermute(grids, MESH, list(enumerate(OWNER)))  7.98 us
    all_to_all x1, waiting for transfers between devices, exchange(): lax.all_to_all(x, MESH, split_axis=0, concat_axis=0, tiled=True, axis_ind...  5.2 us
    ppermute x1, waiting for transfers between devices, body(): west = lax.ppermute(last, MESH, after)  4.01 us
  transfers between devices with their start and end apart: 4, of which 4 were waited for; matrix products, arithmetic and copies ran while one was open for 0% of the time, Pallas kernels for 5%

profile of v5, /device:TPU:1, one launch (start us, length us, event | category | flops | bytes accessed | tf_op | source)
XLA Modules:
  0.0 168.4 jit_solution(11197565187671952664)
XLA Ops:
  0.0 0.0 copy-start.2
  0.0 0.0 copy-start
  0.0 0.0 copy-start.1
  0.0 12.0 %all-to-all-start = ((f32[128,64,128]{2,1,0:T(8,128)}), f32[128,64,128]{2,1,0:T(8,128)}, u32[]{:S(2)}, u32[]{:S(2)}) async-start(f32[128,64,128]{2,1,0:T(8,128)} %bitcast.7), calls=%async_computation | async-start | bytes 8388608 | tf_op jit(solution)/shard_map/all_to_all | solution.py:341
  12.6 0.0 copy-done.2
  12.6 0.0 copy-done
  12.7 0.0 copy-done.1
  12.7 0.3 observations.1
  13.0 8.0 %collective-permute-start = (f32[32,128]{1,0:T(8,128)S(1)}, f32[32,128]{1,0:T(8,128)S(1)}, u32[]{:S(2)}, u32[]{:S(2)}) collective-permute-start(f32[32,128]{1,0:T(8,128)S(1)} %observations.1), channel_id=1, source_target_pairs={{0,0},{1,16},{2,32},{3,48},{4,64},{5,80},{6,96},{7,112},{8,97},{9,... | collective-permute-start | bytes 49160 | tf_op jit(solution)/shard_map/ppermute | solution.py:352
  21.0 36.9 %collective-permute-done.obs_ref = f32[32,128]{1,0:T(8,128)S(1)} collective-permute-done((f32[32,128]{1,0:T(8,128)S(1)}, f32[32,128]{1,0:T(8,128)S(1)}, u32[]{:S(2)}, u32[]{:S(2)}) %collective-permute-start) | collective-permute-done | bytes 16416 | tf_op jit(solution)/shard_map/ppermute | solution.py:352
  57.9 5.2 %all-to-all-done.x_ref = f32[128,64,128]{2,1,0:T(8,128)} async-done(((f32[128,64,128]{2,1,0:T(8,128)}), f32[128,64,128]{2,1,0:T(8,128)}, u32[]{:S(2)}, u32[]{:S(2)}) %all-to-all-start) | async-done | bytes 4194336 | tf_op jit(solution)/shard_map/all_to_all | solution.py:341
  63.1 3.5 %tiles.1 = (f32[64,128,128]{2,1,0:T(8,128)S(1)}, f32[64,32,128]{2,1,0:T(8,128)S(1)}, f32[64,32,128]{2,1,0:T(8,128)S(1)}) custom-call(f32[128,64,128]{2,1,0:T(8,128)} %all-to-all-done.x_ref), custom_call_target="tpu_custom_call" | custom-call | flops 1000000000 | bytes 1048576 | tf_op jit(solution)/shard_map/tiles/pallas_call | solution.py:318
  66.5 2.1 %collective-permute-start.1 = (f32[64,32,128]{2,1,0:T(8,128)S(1)}, f32[64,32,128]{2,1,0:T(8,128)S(1)}, u32[]{:S(2)}, u32[]{:S(2)}) collective-permute-start(f32[64,32,128]{2,1,0:T(8,128)S(1)} %get-tuple-element.24), channel_id=1, source_target_pairs={{0,16},{16,32},{32,48},{48,64},{64,80},{80,96},{96,112},{112,97},{... | collective-permute-start | bytes 3145736 | tf_op jit(solution)/shard_map/ppermute | solution.py:361
  68.6 0.0 collective-permute-start.2
  68.6 3.7 %inner.1 = (f32[64,112,128]{2,1,0:T(8,128)S(1)}, f32[64,96,128]{2,1,0:T(8,128)S(1)}, f32[64,80,128]{2,1,0:T(8,128)S(1)}, f32[64,64,128]{2,1,0:T(8,128)S(1)}) custom-call(f32[64,128,128]{2,1,0:T(8,128)S(1)} %get-tuple-element.20.u_ref), custom_call_target="tpu_custom_call" | custom-call | flops 4000000000 | bytes 1048576 | tf_op jit(solution)/shard_map/inner/pallas_call | solution.py:318
  72.4 4.0 %inner_sums.1 = (f32[512,512]{1,0:T(8,128)S(1)}, f32[512,128]{1,0:T(8,128)S(1)}, f32[8,128]{1,0:T(8,128)S(1)}, bf16[512,1024]{1,0:T(8,128)(2,1)S(1)}, bf16[512,1024]{1,0:T(8,128)(2,1)S(1)}) custom-call(f32[64,64,128]{2,1,0:T(8,128)S(1)} %get-tuple-element.27.inner_ref, f32[32,128]{1,0:T(8,128)S(1)} %collective-permute-done.obs_ref), custom_call_target="tpu_custom_call" | custom-call | flops 6000000000 | bytes 1048576 | tf_op jit(solution)/shard_map/inner_sums/pallas_call | solution.py:318
  76.4 4.0 %collective-permute-done.1.west_ref = f32[64,32,128]{2,1,0:T(8,128)S(1)} collective-permute-done((f32[64,32,128]{2,1,0:T(8,128)S(1)}, f32[64,32,128]{2,1,0:T(8,128)S(1)}, u32[]{:S(2)}, u32[]{:S(2)}) %collective-permute-start.1) | collective-permute-done | bytes 1048608 | tf_op jit(solution)/shard_map/ppermute | solution.py:361
  80.4 2.7 %collective-permute-done.2.east_ref = f32[64,32,128]{2,1,0:T(8,128)S(1)} collective-permute-done((f32[64,32,128]{2,1,0:T(8,128)S(1)}, f32[64,32,128]{2,1,0:T(8,128)S(1)}, u32[]{:S(2)}, u32[]{:S(2)}) %collective-permute-start.2) | collective-permute-done | bytes 1048608 | tf_op jit(solution)/shard_map/ppermute | solution.py:362
  83.1 22.6 %analysis.1 = f32[128,64,128]{2,1,0:T(8,128)S(1)} custom-call(f32[64,128,128]{2,1,0:T(8,128)S(1)} %get-tuple-element.20.u_ref, f32[64,112,128]{2,1,0:T(8,128)S(1)} %get-tuple-element.21.one_ref, f32[64,96,128]{2,1,0:T(8,128)S(1)} %get-tuple-element.22.two_ref, f32[64,80,128]{2,1,0:T(8,128)S(1)} %get-tuple-element.23.three_ref, ...), custom_call_target="tpu_custom_call" | custom-call | flops 30000001024 | bytes 1048576 | tf_op jit(solution)/shard_map/analysis/pallas_call | solution.py:318
  105.7 60.7 %all_to_all.10 = f32[128,64,128]{2,1,0:T(8,128)S(1)} all-to-all(f32[128,64,128]{2,1,0:T(8,128)S(1)} %analysis.1), channel_id=1, replica_groups={{0,16,32,48,64,80,96,112,97,113,1,17,33,49,65,81,66,82,98,114,2,18,34,5..., dimensions={0} | all-to-all | bytes 8388608 | tf_op jit(solution)/shard_map/all_to_all | solution.py:341
  166.3 2.0 %copy.9 = f32[128,64,1,128]{3,2,1,0:T(1,128)} copy(f32[128,64,1,128]{3,2,1,0:T(1,128)S(1)} %bitcast.6) | data formatting | bytes 8388608
  (1 shorter events, 0.0 us)
Async XLA Ops:
  0.0 12.6 %copy-start.2 = (f32[1,2048]{1,0:T(1,128)S(1)}, f32[1,2048]{1,0:T(1,128)}, u32[]{:S(2)}) copy-start(f32[1,2048]{1,0:T(1,128)} %param.8) | copy-start | bytes 24580
  0.0 12.6 %copy-start = (s32[1,2048]{1,0:T(1,128)S(1)}, s32[1,2048]{1,0:T(1,128)}, u32[]{:S(2)}) copy-start(s32[1,2048]{1,0:T(1,128)} %cells_ref.1) | copy-start | bytes 24580
  0.0 12.7 %copy-start.1 = (f32[1,2048]{1,0:T(1,128)S(1)}, f32[1,2048]{1,0:T(1,128)}, u32[]{:S(2)}) copy-start(f32[1,2048]{1,0:T(1,128)} %values_ref.1) | copy-start | bytes 24580
  0.0 63.0 %all-to-all-start = ((f32[128,64,128]{2,1,0:T(8,128)}), f32[128,64,128]{2,1,0:T(8,128)}, u32[]{:S(2)}, u32[]{:S(2)}) async-start(f32[128,64,128]{2,1,0:T(8,128)} %bitcast.7), calls=%async_computation | async-start | bytes 8388608 | tf_op jit(solution)/shard_map/all_to_all | solution.py:341
  13.0 44.9 %collective-permute-start = (f32[32,128]{1,0:T(8,128)S(1)}, f32[32,128]{1,0:T(8,128)S(1)}, u32[]{:S(2)}, u32[]{:S(2)}) collective-permute-start(f32[32,128]{1,0:T(8,128)S(1)} %observations.1), channel_id=1, source_target_pairs={{0,0},{1,16},{2,32},{3,48},{4,64},{5,80},{6,96},{7,112},{8,97},{9,... | collective-permute-start | bytes 49160 | tf_op jit(solution)/shard_map/ppermute | solution.py:352
  66.5 13.8 %collective-permute-start.1 = (f32[64,32,128]{2,1,0:T(8,128)S(1)}, f32[64,32,128]{2,1,0:T(8,128)S(1)}, u32[]{:S(2)}, u32[]{:S(2)}) collective-permute-start(f32[64,32,128]{2,1,0:T(8,128)S(1)} %get-tuple-element.24), channel_id=1, source_target_pairs={{0,16},{16,32},{32,48},{48,64},{64,80},{80,96},{96,112},{112,97},{... | collective-permute-start | bytes 3145736 | tf_op jit(solution)/shard_map/ppermute | solution.py:361
  68.6 14.5 %collective-permute-start.2 = (f32[64,32,128]{2,1,0:T(8,128)S(1)}, f32[64,32,128]{2,1,0:T(8,128)S(1)}, u32[]{:S(2)}, u32[]{:S(2)}) collective-permute-start(f32[64,32,128]{2,1,0:T(8,128)S(1)} %get-tuple-element.25), channel_id=1, source_target_pairs={{16,0},{32,16},{48,32},{64,48},{80,64},{96,80},{112,96},{97,112},{... | collective-permute-start | bytes 3145736 | tf_op jit(solution)/shard_map/ppermute | solution.py:362

commit v6 on v5

--- a/solution.py
+++ b/solution.py
@@ -303,7 +303,7 @@
                 out_ref[pl.ds(place * 8 + ((b + place) & 3) * 2, 2)] = part
         return 0
 
-    lax.fori_loop(0, 8, result_of, 0, unroll=2)
+    lax.fori_loop(0, 8, result_of, 0, unroll=4)
 
 
 def vmem(count):

time: 170 us -> 169 us (level)
  no operation moved by 1% of the time
where the time goes in v6:
time: 169 us; the launch traced here: 168 us
  blocking collectives  60.7 us (36%)
  waiting for transfers between devices  48.8 us (29%)
  Pallas kernels  33.5 us (20%)
  starting transfers between devices  22 us (13%)
  local copies, waits for them, and re-layouts  2.02 us (1%)
    all_to_all x1, blocking collectives, exchange(): lax.all_to_all(x, MESH, split_axis=0, concat_axis=0, tiled=True, axis_ind...  60.7 us
    ppermute x1, waiting for transfers between devices, body(): grids = lax.ppermute(grids, MESH, list(enumerate(OWNER)))  36.9 us
    pallas_call x4, Pallas kernels, call(): pl.pallas_call(kernel, out_shape=[pltpu.VMEM(*out) for out in outs], in_s...  33.2 us
    all_to_all x1, starting transfers between devices, exchange(): lax.all_to_all(x, MESH, split_axis=0, concat_axis=0, tiled=True, axis_ind...  12 us
    ppermute x1, starting transfers between devices, body(): grids = lax.ppermute(grids, MESH, list(enumerate(OWNER)))  7.98 us
    all_to_all x1, waiting for transfers between devices, exchange(): lax.all_to_all(x, MESH, split_axis=0, concat_axis=0, tiled=True, axis_ind...  5.2 us
    ppermute x1, waiting for transfers between devices, body(): west = lax.ppermute(last, MESH, after)  4.01 us
  transfers between devices with their start and end apart: 4, of which 4 were waited for; matrix products, arithmetic and copies ran while one was open for 0% of the time, Pallas kernels for 5%

profile of v6, /device:TPU:1, one launch (start us, length us, event | category | flops | bytes accessed | tf_op | source)
XLA Modules:
  0.0 167.8 jit_solution(17307421277035825869)
XLA Ops:
  0.0 0.0 copy-start.2
  0.0 0.0 copy-start
  0.0 0.0 copy-start.1
  0.0 12.0 %all-to-all-start = ((f32[128,64,128]{2,1,0:T(8,128)}), f32[128,64,128]{2,1,0:T(8,128)}, u32[]{:S(2)}, u32[]{:S(2)}) async-start(f32[128,64,128]{2,1,0:T(8,128)} %bitcast.7), calls=%async_computation | async-start | bytes 8388608 | tf_op jit(solution)/shard_map/all_to_all | solution.py:341
  12.6 0.0 copy-done.2
  12.6 0.0 copy-done
  12.7 0.0 copy-done.1
  12.7 0.3 observations.1
  13.0 8.0 %collective-permute-start = (f32[32,128]{1,0:T(8,128)S(1)}, f32[32,128]{1,0:T(8,128)S(1)}, u32[]{:S(2)}, u32[]{:S(2)}) collective-permute-start(f32[32,128]{1,0:T(8,128)S(1)} %observations.1), channel_id=1, source_target_pairs={{0,0},{1,16},{2,32},{3,48},{4,64},{5,80},{6,96},{7,112},{8,97},{9,... | collective-permute-start | bytes 49160 | tf_op jit(solution)/shard_map/ppermute | solution.py:352
  21.0 36.9 %collective-permute-done.obs_ref = f32[32,128]{1,0:T(8,128)S(1)} collective-permute-done((f32[32,128]{1,0:T(8,128)S(1)}, f32[32,128]{1,0:T(8,128)S(1)}, u32[]{:S(2)}, u32[]{:S(2)}) %collective-permute-start) | collective-permute-done | bytes 16416 | tf_op jit(solution)/shard_map/ppermute | solution.py:352
  57.9 5.2 %all-to-all-done.x_ref = f32[128,64,128]{2,1,0:T(8,128)} async-done(((f32[128,64,128]{2,1,0:T(8,128)}), f32[128,64,128]{2,1,0:T(8,128)}, u32[]{:S(2)}, u32[]{:S(2)}) %all-to-all-start) | async-done | bytes 4194336 | tf_op jit(solution)/shard_map/all_to_all | solution.py:341
  63.1 3.5 %tiles.1 = (f32[64,128,128]{2,1,0:T(8,128)S(1)}, f32[64,32,128]{2,1,0:T(8,128)S(1)}, f32[64,32,128]{2,1,0:T(8,128)S(1)}) custom-call(f32[128,64,128]{2,1,0:T(8,128)} %all-to-all-done.x_ref), custom_call_target="tpu_custom_call" | custom-call | flops 1000000000 | bytes 1048576 | tf_op jit(solution)/shard_map/tiles/pallas_call | solution.py:318
  66.5 2.1 %collective-permute-start.1 = (f32[64,32,128]{2,1,0:T(8,128)S(1)}, f32[64,32,128]{2,1,0:T(8,128)S(1)}, u32[]{:S(2)}, u32[]{:S(2)}) collective-permute-start(f32[64,32,128]{2,1,0:T(8,128)S(1)} %get-tuple-element.24), channel_id=1, source_target_pairs={{0,16},{16,32},{32,48},{48,64},{64,80},{80,96},{96,112},{112,97},{... | collective-permute-start | bytes 3145736 | tf_op jit(solution)/shard_map/ppermute | solution.py:361
  68.6 0.0 collective-permute-start.2
  68.6 3.7 %inner.1 = (f32[64,112,128]{2,1,0:T(8,128)S(1)}, f32[64,96,128]{2,1,0:T(8,128)S(1)}, f32[64,80,128]{2,1,0:T(8,128)S(1)}, f32[64,64,128]{2,1,0:T(8,128)S(1)}) custom-call(f32[64,128,128]{2,1,0:T(8,128)S(1)} %get-tuple-element.20.u_ref), custom_call_target="tpu_custom_call" | custom-call | flops 4000000000 | bytes 1048576 | tf_op jit(solution)/shard_map/inner/pallas_call | solution.py:318
  72.4 4.0 %inner_sums.1 = (f32[512,512]{1,0:T(8,128)S(1)}, f32[512,128]{1,0:T(8,128)S(1)}, f32[8,128]{1,0:T(8,128)S(1)}, bf16[512,1024]{1,0:T(8,128)(2,1)S(1)}, bf16[512,1024]{1,0:T(8,128)(2,1)S(1)}) custom-call(f32[64,64,128]{2,1,0:T(8,128)S(1)} %get-tuple-element.27.inner_ref, f32[32,128]{1,0:T(8,128)S(1)} %collective-permute-done.obs_ref), custom_call_target="tpu_custom_call" | custom-call | flops 6000000000 | bytes 1048576 | tf_op jit(solution)/shard_map/inner_sums/pallas_call | solution.py:318
  76.4 4.0 %collective-permute-done.1.west_ref = f32[64,32,128]{2,1,0:T(8,128)S(1)} collective-permute-done((f32[64,32,128]{2,1,0:T(8,128)S(1)}, f32[64,32,128]{2,1,0:T(8,128)S(1)}, u32[]{:S(2)}, u32[]{:S(2)}) %collective-permute-start.1) | collective-permute-done | bytes 1048608 | tf_op jit(solution)/shard_map/ppermute | solution.py:361
  80.4 2.7 %collective-permute-done.2.east_ref = f32[64,32,128]{2,1,0:T(8,128)S(1)} collective-permute-done((f32[64,32,128]{2,1,0:T(8,128)S(1)}, f32[64,32,128]{2,1,0:T(8,128)S(1)}, u32[]{:S(2)}, u32[]{:S(2)}) %collective-permute-start.2) | collective-permute-done | bytes 1048608 | tf_op jit(solution)/shard_map/ppermute | solution.py:362
  83.1 22.0 %analysis.1 = f32[128,64,128]{2,1,0:T(8,128)S(1)} custom-call(f32[64,128,128]{2,1,0:T(8,128)S(1)} %get-tuple-element.20.u_ref, f32[64,112,128]{2,1,0:T(8,128)S(1)} %get-tuple-element.21.one_ref, f32[64,96,128]{2,1,0:T(8,128)S(1)} %get-tuple-element.22.two_ref, f32[64,80,128]{2,1,0:T(8,128)S(1)} %get-tuple-element.23.three_ref, ...), custom_call_target="tpu_custom_call" | custom-call | flops 30000001024 | bytes 1048576 | tf_op jit(solution)/shard_map/analysis/pallas_call | solution.py:318
  105.1 60.7 %all_to_all.10 = f32[128,64,128]{2,1,0:T(8,128)S(1)} all-to-all(f32[128,64,128]{2,1,0:T(8,128)S(1)} %analysis.1), channel_id=1, replica_groups={{0,16,32,48,64,80,96,112,97,113,1,17,33,49,65,81,66,82,98,114,2,18,34,5..., dimensions={0} | all-to-all | bytes 8388608 | tf_op jit(solution)/shard_map/all_to_all | solution.py:341
  165.8 2.0 %copy.9 = f32[128,64,1,128]{3,2,1,0:T(1,128)} copy(f32[128,64,1,128]{3,2,1,0:T(1,128)S(1)} %bitcast.6) | data formatting | bytes 8388608
  (1 shorter events, 0.0 us)
Async XLA Ops:
  0.0 12.6 %copy-start.2 = (f32[1,2048]{1,0:T(1,128)S(1)}, f32[1,2048]{1,0:T(1,128)}, u32[]{:S(2)}) copy-start(f32[1,2048]{1,0:T(1,128)} %param.8) | copy-start | bytes 24580
  0.0 12.6 %copy-start = (s32[1,2048]{1,0:T(1,128)S(1)}, s32[1,2048]{1,0:T(1,128)}, u32[]{:S(2)}) copy-start(s32[1,2048]{1,0:T(1,128)} %cells_ref.1) | copy-start | bytes 24580
  0.0 12.7 %copy-start.1 = (f32[1,2048]{1,0:T(1,128)S(1)}, f32[1,2048]{1,0:T(1,128)}, u32[]{:S(2)}) copy-start(f32[1,2048]{1,0:T(1,128)} %values_ref.1) | copy-start | bytes 24580
  0.0 63.0 %all-to-all-start = ((f32[128,64,128]{2,1,0:T(8,128)}), f32[128,64,128]{2,1,0:T(8,128)}, u32[]{:S(2)}, u32[]{:S(2)}) async-start(f32[128,64,128]{2,1,0:T(8,128)} %bitcast.7), calls=%async_computation | async-start | bytes 8388608 | tf_op jit(solution)/shard_map/all_to_all | solution.py:341
  13.0 44.9 %collective-permute-start = (f32[32,128]{1,0:T(8,128)S(1)}, f32[32,128]{1,0:T(8,128)S(1)}, u32[]{:S(2)}, u32[]{:S(2)}) collective-permute-start(f32[32,128]{1,0:T(8,128)S(1)} %observations.1), channel_id=1, source_target_pairs={{0,0},{1,16},{2,32},{3,48},{4,64},{5,80},{6,96},{7,112},{8,97},{9,... | collective-permute-start | bytes 49160 | tf_op jit(solution)/shard_map/ppermute | solution.py:352
  66.5 13.8 %collective-permute-start.1 = (f32[64,32,128]{2,1,0:T(8,128)S(1)}, f32[64,32,128]{2,1,0:T(8,128)S(1)}, u32[]{:S(2)}, u32[]{:S(2)}) collective-permute-start(f32[64,32,128]{2,1,0:T(8,128)S(1)} %get-tuple-element.24), channel_id=1, source_target_pairs={{0,16},{16,32},{32,48},{48,64},{64,80},{80,96},{96,112},{112,97},{... | collective-permute-start | bytes 3145736 | tf_op jit(solution)/shard_map/ppermute | solution.py:361
  68.6 14.5 %collective-permute-start.2 = (f32[64,32,128]{2,1,0:T(8,128)S(1)}, f32[64,32,128]{2,1,0:T(8,128)S(1)}, u32[]{:S(2)}, u32[]{:S(2)}) collective-permute-start(f32[64,32,128]{2,1,0:T(8,128)S(1)} %get-tuple-element.25), channel_id=1, source_target_pairs={{16,0},{32,16},{48,32},{64,48},{80,64},{96,80},{112,96},{97,112},{... | collective-permute-start | bytes 3145736 | tf_op jit(solution)/shard_map/ppermute | solution.py:362
